TPU v7x, 256 devices: a whole 4x4x8 slice. The times are simulated.
256 devices in a mesh: grp: 4 (over y_hi, core), blk: 64 (over z, y_lo, x).
Axes of the slice: x: 4, y: 4 (y_hi: 2, y_lo: 2; y = y_hi * 2 + y_lo), z: 8, core: 2. Of those that a mesh axis runs over, the one named last changes fastest.
Arguments:
- image_embed: bfloat16 [8192, 1152], P(('grp', 'blk')), may hold values from -0.53033009 to 0.53033009
- text_feature: bfloat16 [8192, 1152], P(('grp', 'blk')), may hold values from -0.18 to 0.18
- text_head: bfloat16 [1152, 1152], replicated, may hold values from -0.176776695 to 0.176776695
- log_scale: float32 [1], replicated, may hold values from 4 to 4.8
- bias: float32 [1], replicated, may hold values from -10 to -6
Outputs:
- grad_image: bfloat16 [8192, 1152], P(('grp', 'blk'))
- grad_text: bfloat16 [8192, 1152], P(('grp', 'blk'))
- grad_head: float32 [1152, 1152], P('blk')
All inputs are finite; a program needn't handle non-finite values.
Results may differ from a plain program's by a relative error of at most 0.018.
Values may be sent and summed in bfloat16 or wider, within the bound.
A program may use at most 64 MiB of HBM per device.

v0:
```python
import jax
import jax.numpy as jnp
from jax import lax
from jax.sharding import Mesh
from jax.sharding import PartitionSpec as P

BLK = ("blk_0", "blk_1", "blk_2")
GRP_BLK = ("grp", "blk_0", "blk_1", "blk_2")


EPSILON = 1e-06


def sent_to_all(value, axis):
    peers = lax.axis_size(axis)
    return lax.all_to_all(
        jnp.broadcast_to(value[None], (peers, *value.shape)), axis, 0, 0, tiled=True
    )


def joined_along(parts, dim):
    dims = list(parts.shape[1:])
    dims[dim] *= parts.shape[0]
    return jnp.moveaxis(parts, 0, dim).reshape(dims)


def gather_directly(value, axis, dim):
    parts = sent_to_all(value, axis)
    return joined_along(parts, dim)


def all_blocks(value, axes, turns):
    parts = value
    for k in turns:
        parts = lax.all_gather(parts, axes[k])
    done = turns[::-1]
    back = [done.index(k) for k in range(len(axes))]
    parts = parts.transpose(*back, *range(len(axes), parts.ndim))
    return parts.reshape(-1, *value.shape)


def whole_of(value, axes, turns, dim):
    return joined_along(all_blocks(value, axes, turns), dim)


def own_block(parts, axes, turns):
    dims = [lax.axis_size(a) for a in axes]
    parts = parts.reshape(*dims, *parts.shape[1:])
    parts = parts.transpose(*turns, *range(len(axes), parts.ndim))
    parts = parts.reshape(-1, *parts.shape[len(axes) :])
    for k in turns:
        parts = lax.psum_scatter(parts, axes[k], scatter_dimension=0, tiled=True)
    return parts[0]


def cut_along(value, dim, peers):
    dims = value.shape
    parts = value.reshape(*dims[:dim], peers, dims[dim] // peers, *dims[dim + 1 :])
    return jnp.moveaxis(parts, dim, 0)


def summed_rows(value, axes, turns, dim):
    peers = lax.axis_size(axes)
    return own_block(cut_along(value, dim, peers), axes, turns)


def sent_and_summed(value, axis, dim):
    peers = lax.axis_size(axis)
    parts = lax.all_to_all(cut_along(value, dim, peers), axis, 0, 0, tiled=True)
    return jnp.sum(parts.astype(jnp.float32), axis=0)


def sum_by_axis(value, axes, dim):
    far, near = axes
    parts = cut_along(value, dim, lax.axis_size(far))
    nearer = sent_and_summed(parts, near, dim + 1)
    arrived = lax.all_to_all(
        nearer.astype(jnp.bfloat16), far, split_axis=0, concat_axis=0, tiled=True
    )
    return arrived.astype(jnp.float32).sum(axis=0)


def over_copies(value, axis):
    return sent_to_all(value, axis).astype(jnp.float32).sum(axis=0)


def normalized(values):
    widened = values.astype(jnp.float32)
    length = jnp.sqrt(jnp.sum(widened * widened, axis=-1, keepdims=True) + EPSILON)
    return (widened / length, length)


def local(image_embed, text_feature, text_head, log_scale, bias):
    shard_rows = image_embed.shape[0]
    cycle_size = lax.axis_size(BLK)
    group_size = lax.axis_size("grp")
    my_block = lax.axis_index(BLK)
    my_group = lax.axis_index("grp")
    image_dir, image_len = normalized(image_embed)
    image_low = image_dir.astype(jnp.bfloat16)
    projected = jnp.dot(text_feature, text_head, preferred_element_type=jnp.float32)
    text_dir, text_len = normalized(projected)
    text_low = text_dir.astype(jnp.bfloat16)
    factor = jnp.exp(log_scale[0])
    offset = bias[0]
    gathered = gather_directly(image_low, "grp", 0)
    local_ids = jnp.arange(group_size * shard_rows, dtype=jnp.int32)
    image_ids = (
        local_ids // shard_rows * cycle_size + my_block
    ) * shard_rows + local_ids % shard_rows
    text_all = whole_of(text_low, BLK, (1, 0, 2), 0)
    all_ids = my_group * cycle_size * shard_rows + jnp.arange(
        cycle_size * shard_rows, dtype=jnp.int32
    )
    logits = (
        factor
        * lax.dot_general(
            gathered, text_all, (((1,), (1,)), ((), ())), preferred_element_type=jnp.float32
        )
        + offset
    )
    matched = (image_ids[:, None] == all_ids[None, :]).astype(jnp.float32)
    weights = (factor * (jax.nn.sigmoid(logits) - matched)).astype(jnp.bfloat16)
    image_part = jnp.dot(weights, text_all, preferred_element_type=jnp.float32)
    text_part = lax.dot_general(
        weights, gathered, (((0,), (0,)), ((), ())), preferred_element_type=jnp.float32
    )
    text_sum = summed_rows(text_part.astype(jnp.bfloat16), BLK, (0, 2, 1), 0).astype(jnp.float32)
    image_sum = sent_and_summed(image_part.astype(jnp.bfloat16), "grp", 0)
    grad_image = (
        (image_sum - image_dir * jnp.sum(image_dir * image_sum, axis=-1, keepdims=True)) / image_len
    ).astype(jnp.bfloat16)
    proj_grad = (
        (text_sum - text_dir * jnp.sum(text_dir * text_sum, axis=-1, keepdims=True)) / text_len
    ).astype(jnp.bfloat16)
    grad_text = lax.dot_general(
        proj_grad, text_head, (((1,), (1,)), ((), ())), preferred_element_type=jnp.float32
    ).astype(jnp.bfloat16)
    head_share = sum_by_axis(
        lax.dot_general(
            text_feature, proj_grad, (((0,), (0,)), ((), ())), preferred_element_type=jnp.float32
        ).astype(jnp.bfloat16),
        (("blk_0", "blk_1"), "blk_2"),
        0,
    )
    grad_head = over_copies(head_share.astype(jnp.bfloat16), "grp").astype(jnp.float32)
    return (grad_image, grad_text, grad_head)


def solution(mesh):
    torus = Mesh(
        mesh.devices.reshape(mesh.shape["grp"], 8, 2, 4), ("grp", "blk_0", "blk_1", "blk_2")
    )
    return jax.shard_map(
        local,
        mesh=torus,
        in_specs=(P(GRP_BLK, None), P(GRP_BLK, None), P(), P(), P()),
        out_specs=(P(GRP_BLK, None), P(GRP_BLK, None), P(BLK, None)),
        check_vma=False,
    )
```

profile of v0, /device:TPU:1, one launch (start us, length us, event | category | flops | bytes accessed | tf_op | source)
XLA Modules:
  0.0 346.6 jit_solution(15468163740864732396)
XLA Ops:
  7.2 1.7 copy-done
  8.9 1.6 multiply_reduce_fusion.1
  10.6 4.6 %all-gather = bf16[64,1152]{1,0:T(8,128)(2,1)} all-gather(bf16[32,1152]{1,0:T(8,128)(2,1)S(1)} %fusion.18), channel_id=2, replica_groups=mesh['grp'=4,'blk_0'=8,'blk_1'=2,'blk_2'=4] {'blk_1'}, dimensions={0}, use_global_device_ids=true | all-gather | bytes 221184 | tf_op jit(solution)/shard_map/all_gather | solution.py:35
  15.3 38.2 %all-gather.6.cloned.1.call-done = bf16[16,32,1152]{2,1,0:T(8,128)(2,1)} async-done(((bf16[2,32,1152]{2,1,0:T(8,128)(2,1)}), bf16[16,32,1152]{2,1,0:T(8,128)(2,1)}) %all-gather.6.cloned.1.call-update) | async-done | bytes 1179664 | tf_op jit(solution)/shard_map/all_gather | solution.py:35
  53.6 1.0 fusion.9
  55.4 10.0 %all-to-all-start = ((bf16[4,32,1152]{2,1,0:T(8,128)(2,1)}), bf16[4,32,1152]{2,1,0:T(8,128)(2,1)S(1)}, u32[]{:S(2)}, u32[]{:S(2)}) async-start(bf16[4,32,1152]{2,1,0:T(8,128)(2,1)} %broadcast_in_dim.4), calls=%async_computation | async-start | bytes 589824 | tf_op jit(solution)/shard_map/all_to_all | solution.py:16
  66.8 46.9 %all-gather.8.cloned.1.call-done = bf16[32,2,32,1152]{3,2,1,0:T(8,128)(2,1)} async-done(((bf16[8,2,32,1152]{3,2,1,0:T(8,128)(2,1)}), bf16[32,2,32,1152]{3,2,1,0:T(8,128)(2,1)}) %all-gather.8.cloned.1.call-update) | async-done | bytes 4718608 | tf_op jit(solution)/shard_map/all_gather | solution.py:35
  113.7 5.0 %copy.26 = bf16[8,2,4,32,1152]{4,3,2,1,0:T(8,128)(2,1)} copy(bf16[8,2,4,32,1152]{4,3,1,0,2:T(8,128)(2,1)} %bitcast.39) | data formatting | bytes 9437184 | tf_op jit(solution)/shard_map/transpose | solution.py:38
  119.4 4.2 %fusion.8 = bf16[128,2048]{1,0:T(8,128)(2,1)S(1)} fusion(bf16[128,1152]{1,0:T(8,128)(2,1)} %bitcast.40, bf16[2048,1152]{1,0:T(8,128)(2,1)} %bitcast.35, s32[2048]{0:T(1024)S(1)} %iota_add_fusion, f32[]{:T(128)} %bitcast.33, f32[]{:T(128)} %bitcast, s32[128]{0:T(128)S(1)} %fusion.13), kind=kOutput, calls=%fused_computation.11 | convolution fusion | flops 606601216 | bytes 5546504 | tf_op jit(solution)/shard_map/dot_general | solution.py:117
  123.6 1.4 convolution_convert_fusion.1
  125.0 2.8 copy.27
  127.9 60.9 %reduce-scatter.4.cloned.1.call-done = bf16[8,32,1152]{2,1,0:T(8,128)(2,1)} async-done(((bf16[64,32,1152]{2,1,0:T(8,128)(2,1)}), bf16[8,32,1152]{2,1,0:T(8,128)(2,1)}) %reduce-scatter.4.cloned.1.call-update) | async-done | bytes 589840 | tf_op jit(solution)/shard_map/reduce_scatter | solution.py:52
  188.9 23.5 %reduce-scatter.6.cloned.1.call-done = bf16[2,32,1152]{2,1,0:T(8,128)(2,1)} async-done(((bf16[8,32,1152]{2,1,0:T(8,128)(2,1)}), bf16[2,32,1152]{2,1,0:T(8,128)(2,1)}) %reduce-scatter.6.cloned.1.call-update) | async-done | bytes 147472 | tf_op jit(solution)/shard_map/reduce_scatter | solution.py:52
  212.5 19.4 %reduce-scatter.8.cloned.1.call-done = bf16[1,32,1152]{2,1,0:T(8,128)(2,1)} async-done(((bf16[2,32,1152]{2,1,0:T(8,128)(2,1)}), bf16[1,32,1152]{2,1,0:T(8,128)(2,1)}) %reduce-scatter.8.cloned.1.call-update) | async-done | bytes 73744 | tf_op jit(solution)/shard_map/reduce_scatter | solution.py:52
  231.9 1.1 fusion.10
  233.0 3.4 fusion
  236.4 5.3 %reshape_reshape.11 = bf16[16,4,18,1152]{3,2,1,0:T(8,128)(2,1)} reshape(bf16[1152,1152]{1,0:T(8,128)(2,1)} %fusion) | data formatting | bytes 5308416 | tf_op jit(solution)/shard_map/reshape;reshape | solution.py:58
  241.7 4.4 %copy.28 = bf16[4,16,18,1152]{3,1,2,0:T(8,128)(2,1)} copy(bf16[4,16,18,1152]{3,2,0,1:T(8,128)(2,1)} %bitcast.38) | data formatting | bytes 5308416 | tf_op jit(solution)/shard_map/transpose | solution.py:59
  246.1 4.5 %all-to-all-start.2 = ((bf16[4,16,18,1152]{3,1,2,0:T(8,128)(2,1)}), bf16[4,16,18,1152]{3,1,2,0:T(8,128)(2,1)}, u32[]{:S(2)}, u32[]{:S(2)}) async-start(bf16[4,16,18,1152]{3,1,2,0:T(8,128)(2,1)} %copy.28), calls=%async_computation.5 | async-start | bytes 5308416 | tf_op jit(solution)/shard_map/all_to_all | solution.py:69
  250.7 3.9 %convolution_convert_fusion.2 = bf16[128,1152]{1,0:T(8,128)(2,1)} fusion(bf16[128,2048]{1,0:T(8,128)(2,1)S(1)} %fusion.8, bf16[2048,1152]{1,0:T(8,128)(2,1)} %bitcast.36), kind=kOutput, calls=%fused_computation.12 | convolution fusion | flops 604127232 | bytes 5537792 | tf_op jit(solution)/shard_map/dot_general | solution.py:124
  254.6 27.7 %all-to-all-done.2 = bf16[4,16,18,1152]{3,1,2,0:T(8,128)(2,1)} async-done(((bf16[4,16,18,1152]{3,1,2,0:T(8,128)(2,1)}), bf16[4,16,18,1152]{3,1,2,0:T(8,128)(2,1)}, u32[]{:S(2)}, u32[]{:S(2)}) %all-to-all-start.2) | async-done | bytes 2654240 | tf_op jit(solution)/shard_map/all_to_all | solution.py:69
  282.2 5.7 %all-to-all-start.1 = ((bf16[4,32,1152]{2,1,0:T(8,128)(2,1)}), bf16[4,32,1152]{2,1,0:T(8,128)(2,1)S(1)}, u32[]{:S(2)}, u32[]{:S(2)}) async-start(bf16[4,32,1152]{2,1,0:T(8,128)(2,1)} %bitcast.43), calls=%async_computation.1 | async-start | bytes 589824 | tf_op jit(solution)/shard_map/all_to_all | solution.py:69
  288.0 3.2 reduce_sum.83
  291.2 2.1 copy.29
  293.3 1.5 all-to-all-done.1
  294.9 6.9 %all-to-all-start.3 = ((bf16[16,18,1152]{2,1,0:T(8,128)(2,1)}), bf16[16,18,1152]{2,1,0:T(8,128)(2,1)}, u32[]{:S(2)}, u32[]{:S(2)}) async-start(bf16[16,18,1152]{2,1,0:T(8,128)(2,1)} %copy.29), calls=%async_computation.6 | async-start | bytes 1769472 | tf_op jit(solution)/shard_map/all_to_all | solution.py:77
  302.0 0.7 divide_convert_fusion
  302.7 21.3 %all-to-all-done.3 = bf16[16,18,1152]{2,1,0:T(8,128)(2,1)} async-done(((bf16[16,18,1152]{2,1,0:T(8,128)(2,1)}), bf16[16,18,1152]{2,1,0:T(8,128)(2,1)}, u32[]{:S(2)}, u32[]{:S(2)}) %all-to-all-start.3) | async-done | bytes 663584 | tf_op jit(solution)/shard_map/all_to_all | solution.py:77
  324.0 1.3 reduce_sum.84
  326.0 7.3 %all-to-all-start.4 = ((bf16[4,18,1152]{2,1,0:T(8,128)(2,1)}), bf16[4,18,1152]{2,1,0:T(8,128)(2,1)S(1)}, u32[]{:S(2)}, u32[]{:S(2)}) async-start(bf16[4,18,1152]{2,1,0:T(8,128)(2,1)} %broadcast_in_dim.5), calls=%async_computation.7 | async-start | bytes 442368 | tf_op jit(solution)/shard_map/all_to_all | solution.py:16
  333.3 1.5 convolution_convert_fusion.3
  334.8 4.6 %all-to-all-done.4 = bf16[4,18,1152]{2,1,0:T(8,128)(2,1)S(1)} async-done(((bf16[4,18,1152]{2,1,0:T(8,128)(2,1)}), bf16[4,18,1152]{2,1,0:T(8,128)(2,1)S(1)}, u32[]{:S(2)}, u32[]{:S(2)}) %all-to-all-start.4) | async-done | bytes 165920 | tf_op jit(solution)/shard_map/all_to_all | solution.py:16
  (33 shorter events, 3.5 us)
Async XLA Ops:
  7.2 1.8 copy-start
  7.2 47.4 %copy-start.3 = (bf16[32,1152]{1,0:T(8,128)(2,1)S(1)}, bf16[32,1152]{1,0:T(8,128)(2,1)}, u32[]{:S(2)}) copy-start(bf16[32,1152]{1,0:T(8,128)(2,1)} %param.5) | copy-start | bytes 221188
  7.2 46.3 %all-gather.6.cloned.1.call-start = ((), (), s32[]{:S(2)}) async-start(), calls=%async_computation.11 | async-start | bytes 1327104 | tf_op jit(solution)/shard_map/all_gather | solution.py:35
  15.2 98.5 %all-gather.8.cloned.1.call-start = ((), (), s32[]{:S(2)}) async-start(), calls=%async_computation.12 | async-start | bytes 5898240 | tf_op jit(solution)/shard_map/all_gather | solution.py:35
  55.4 63.3 %all-to-all-start = ((bf16[4,32,1152]{2,1,0:T(8,128)(2,1)}), bf16[4,32,1152]{2,1,0:T(8,128)(2,1)S(1)}, u32[]{:S(2)}, u32[]{:S(2)}) async-start(bf16[4,32,1152]{2,1,0:T(8,128)(2,1)} %broadcast_in_dim.4), calls=%async_computation | async-start | bytes 589824 | tf_op jit(solution)/shard_map/all_to_all | solution.py:16
  65.4 123.5 %reduce-scatter.4.cloned.1.call-start = ((), (), s32[]{:S(2)}) async-start(), calls=%async_computation.8 | async-start | bytes 5308416 | tf_op jit(solution)/shard_map/reduce_scatter | solution.py:52
  118.7 0.7 copy-start.1
  119.4 4.2 %copy-start.2 = (bf16[4,32,1152]{2,1,0:T(8,128)(2,1)S(1)}, bf16[4,32,1152]{2,1,0:T(8,128)(2,1)}, u32[]{:S(2)}) copy-start(bf16[4,32,1152]{2,1,0:T(8,128)(2,1)} %copy-done.1) | copy-start | bytes 884740
  127.8 105.1 %copy-start.5 = (bf16[32,1152]{1,0:T(8,128)(2,1)S(1)}, bf16[32,1152]{1,0:T(8,128)(2,1)}, u32[]{:S(2)}) copy-start(bf16[32,1152]{1,0:T(8,128)(2,1)} %param.6) | copy-start | bytes 221188
  127.9 84.6 %reduce-scatter.6.cloned.1.call-start = ((), (), s32[]{:S(2)}) async-start(), calls=%async_computation.9 | async-start | bytes 737280 | tf_op jit(solution)/shard_map/reduce_scatter | solution.py:52
  188.9 43.0 %reduce-scatter.8.cloned.1.call-start = ((), (), s32[]{:S(2)}) async-start(), calls=%async_computation.10 | async-start | bytes 221184 | tf_op jit(solution)/shard_map/reduce_scatter | solution.py:52
  246.1 36.1 %all-to-all-start.2 = ((bf16[4,16,18,1152]{3,1,2,0:T(8,128)(2,1)}), bf16[4,16,18,1152]{3,1,2,0:T(8,128)(2,1)}, u32[]{:S(2)}, u32[]{:S(2)}) async-start(bf16[4,16,18,1152]{3,1,2,0:T(8,128)(2,1)} %copy.28), calls=%async_computation.5 | async-start | bytes 5308416 | tf_op jit(solution)/shard_map/all_to_all | solution.py:69
  282.2 12.6 %all-to-all-start.1 = ((bf16[4,32,1152]{2,1,0:T(8,128)(2,1)}), bf16[4,32,1152]{2,1,0:T(8,128)(2,1)S(1)}, u32[]{:S(2)}, u32[]{:S(2)}) async-start(bf16[4,32,1152]{2,1,0:T(8,128)(2,1)} %bitcast.43), calls=%async_computation.1 | async-start | bytes 589824 | tf_op jit(solution)/shard_map/all_to_all | solution.py:69
  288.0 45.3 %copy-start.4 = (bf16[1,32,1152]{2,1,0:T(8,128)(2,1)S(1)}, bf16[1,32,1152]{2,1,0:T(8,128)(2,1)}, u32[]{:S(2)}) copy-start(bf16[1,32,1152]{2,1,0:T(8,128)(2,1)} %reduce-scatter.8.cloned.1.call-done) | copy-start | bytes 221188
  294.9 29.1 %all-to-all-start.3 = ((bf16[16,18,1152]{2,1,0:T(8,128)(2,1)}), bf16[16,18,1152]{2,1,0:T(8,128)(2,1)}, u32[]{:S(2)}, u32[]{:S(2)}) async-start(bf16[16,18,1152]{2,1,0:T(8,128)(2,1)} %copy.29), calls=%async_computation.6 | async-start | bytes 1769472 | tf_op jit(solution)/shard_map/all_to_all | solution.py:77
  326.0 13.4 %all-to-all-start.4 = ((bf16[4,18,1152]{2,1,0:T(8,128)(2,1)}), bf16[4,18,1152]{2,1,0:T(8,128)(2,1)S(1)}, u32[]{:S(2)}, u32[]{:S(2)}) async-start(bf16[4,18,1152]{2,1,0:T(8,128)(2,1)} %broadcast_in_dim.5), calls=%async_computation.7 | async-start | bytes 442368 | tf_op jit(solution)/shard_map/all_to_all | solution.py:16
Sparse Core Ops, SparseCore 0:
  15.4 38.1 all-gather.5
  55.3 58.3 all-gather.7
  128.0 60.8 reduce-scatter.3
  191.2 21.1 reduce-scatter.5
  214.8 17.0 reduce-scatter.7
where the time goes:
time: 348 us; the launch traced here: 347 us
  waiting for transfers between devices  244 us (70%)
  starting transfers between devices  34.5 us (10%)
  local copies, waits for them, and re-layouts  23.6 us (7%)
  matrix products  16 us (5%)
  between operations  15.2 us (4%)
  other arithmetic  8.45 us (2%)
  blocking collectives  4.61 us (1%)
    reduce_scatter x3, waiting for transfers between devices, own_block(): parts = lax.psum_scatter(parts, axes[k], scatter_dimension=0, tiled=True)  104 us
    all_gather x2, waiting for transfers between devices, all_blocks(): parts = lax.all_gather(parts, axes[k])  85.2 us
    all_to_all x2, waiting for transfers between devices, sent_and_summed(): parts = lax.all_to_all(cut_along(value, dim, peers), axis, 0, 0, tiled=True)  29.2 us
    all_to_all x1, waiting for transfers between devices, sum_by_axis(): lax.all_to_all(nearer.astype(jnp.bfloat16), far, split_axis=0, concat_axi...  21.3 us
    all_to_all x2, starting transfers between devices, sent_to_all(): lax.all_to_all(jnp.broadcast_to(value[None], (peers, *value.shape)), axis...  17.2 us
    all_to_all x2, starting transfers between devices, sent_and_summed(): parts = lax.all_to_all(cut_along(value, dim, peers), axis, 0, 0, tiled=True)  10.3 us
  transfers between devices with their start and end apart: 10, of which 9 were waited for; matrix products, arithmetic and copies ran while one was open for 5% of the time, Pallas kernels for 0%

commit v1 on v0

v1 whole, which is shorter than its diff:
```python
import jax
import jax.numpy as jnp
from jax import lax
from jax.experimental import pallas as pl
from jax.experimental.pallas import tpu as pltpu
from jax.sharding import PartitionSpec as P

MESH = pl.DeviceIdType.MESH
EPSILON = 1e-06
F32 = jnp.float32
BF16 = jnp.bfloat16
D = 1152
ROWS = 32
HALF = 16
NX, NY, NZ, NK = 4, 4, 8, 2
ALL = 512
COLS = D // NZ
SLICE = 18


def place():
    grp = lax.axis_index("grp")
    blk = lax.axis_index("blk")
    return blk % 4, (grp // 2) * 2 + (blk // 4) % 2, blk // 8, grp % 2


def device(x, y, z, k):
    return ((y // 2) * 2 + k, z * 8 + (y % 2) * 4 + x)


def rows(start, count):
    return pl.ds(start, count)


def kernel(
    scale_ref, bias_ref, image_ref, text_ref, fsel_ref, head_hbm,
    gi_ref, gt_ref, gh_ref,
    head, img, txt, wt, tp, ip, tpd, rz, iay, iax, ibx, iby,
    tdir, pall, fall, hp, hm, hl, rm, rl, sm, sl, qm, ql,
    head_sem, s_img, r_img, s_z, r_z, s_k, r_k, s_f, r_f, s_rs, r_rs, s_ir, r_ir,
    s_p, r_p, s_h, r_h, s_q, r_q,
):
    x, y, z, k = place()

    def at(dx=0, dy=0, dz=0, dk=0):
        return device((x + dx) % NX, (y + dy) % NY, (z + dz) % NZ, (k + dk) % NK)

    sent = []

    def send(src, dst, ssem, rsem, where):
        copy = pltpu.make_async_remote_copy(
            src_ref=src, dst_ref=dst, send_sem=ssem, recv_sem=rsem,
            device_id=where, device_id_type=MESH,
        )
        copy.start()
        sent.append(copy)
        return copy

    load = pltpu.make_async_copy(head_hbm, head, head_sem)
    load.start()

    barrier = pltpu.get_barrier_semaphore()
    partners = (
        [dict(dx=i) for i in (1, 2, 3)]
        + [dict(dy=i) for i in (1, 2, 3)]
        + [dict(dz=i) for i in range(1, 8)]
        + [dict(dy=i, dk=1) for i in range(4)]
        + [dict(dx=i, dk=1) for i in (1, 2, 3)]
    )
    for p in partners:
        pl.semaphore_signal(barrier, inc=1, device_id=at(**p), device_id_type=MESH)

    wide = image_ref[...].astype(F32)
    image_len = jnp.sqrt(jnp.sum(wide * wide, axis=-1, keepdims=True) + EPSILON)
    low = (wide / image_len).astype(BF16)
    img[rows(0, HALF), :] = low[:HALF]
    img[rows(256, HALF), :] = low[HALF:]

    pl.semaphore_wait(barrier, len(partners))

    ca, cb = {}, {}

    def send_a(dx, dy, sx):
        src = img.at[rows(sx * HALF, HALF), :]
        tx, ty = dx, dy
        slot = ty * 4 + tx
        return src, img.at[rows(slot * HALF, HALF), :], slot

    def ship_a(tx, ty, sx, where):
        src = img.at[rows(sx * HALF, HALF), :]
        slot = ty * 4 + tx
        ca[(tx, ty)] = send(src, img.at[rows(slot * HALF, HALF), :],
                            s_img.at[slot], r_img.at[slot], where)

    def ship_b(tx, ty, sy, where):
        src = img.at[rows(256 + sy * HALF, HALF), :]
        slot = tx * 4 + ty
        cb[(tx, ty)] = send(src, img.at[rows(256 + slot * HALF, HALF), :],
                            s_img.at[16 + slot], r_img.at[16 + slot], where)

    order = (1, 3, 2)
    for i in order:
        ship_a(4 - i, 0, 0, at(dx=i))
        ship_b(0, 4 - i, 0, at(dy=i))
    for i in order:
        ship_a(0, 4 - i, 0, at(dy=i))
        ship_b(4 - i, 0, 0, at(dx=i))

    fall[0] = fsel_ref[k * 4 + x]
    cf = {}
    for dk in range(2):
        for dx in range(4):
            if dk == 0 and dx == 0:
                continue
            slot = ((4 - dx) % 4) + 4 * dk
            cf[slot] = send(fsel_ref.at[((k + dk) % 2) * 4 + (x + dx) % 4], fall.at[slot],
                            s_f.at[slot], r_f.at[slot], at(dx=dx, dk=dk))

    load.wait()
    projected = jnp.dot(text_ref[...], head[...], preferred_element_type=F32)
    text_len = jnp.sqrt(jnp.sum(projected * projected, axis=-1, keepdims=True) + EPSILON)
    text_dir = projected / text_len
    tdir[...] = text_dir
    txt[rows(0, ROWS), :] = text_dir.astype(BF16)

    cz = {}

    def ship_z(sign, step, half):
        src_slot = ((8 - (step - 1)) % 8) if sign > 0 else step - 1
        dst_slot = (8 - step) if sign > 0 else step
        n = ((0 if sign > 0 else 4) + step - 1) * 2 + half
        cz[(sign, step, half)] = send(
            txt.at[rows(src_slot * ROWS + half * HALF, HALF), :],
            txt.at[rows(dst_slot * ROWS + half * HALF, HALF), :],
            s_z.at[n], r_z.at[n], at(dz=sign))

    ck = {}

    def ship_k(slot):
        ck[slot] = send(txt.at[rows(slot * ROWS, ROWS), :], txt.at[rows(256 + slot * ROWS, ROWS), :],
                        s_k.at[slot], r_k.at[slot], at(dk=1))

    for half in range(2):
        ship_z(1, 1, half)
        ship_z(-1, 1, half)
    ship_k(0)

    def forward_image(i):
        ca[(i, 0)].wait_recv()
        for j in order:
            ship_a(i, 4 - j, i, at(dy=j))
        cb[(0, i)].wait_recv()
        for j in order:
            ship_b(4 - j, i, i, at(dx=j))

    forward_image(3)
    forward_image(1)
    for step in (1, 2, 3):
        for half in range(2):
            cz[(1, step, half)].wait_recv()
            if step < 3 or half == 0:
                ship_z(1, step + 1, half)
            cz[(-1, step, half)].wait_recv()
            if step < 3 or half == 1:
                ship_z(-1, step + 1, half)
        ship_k(8 - step)
        ship_k(step)
        if step == 1:
            forward_image(2)
    cz[(1, 4, 0)].wait_recv()
    cz[(-1, 4, 1)].wait_recv()
    ship_k(4)

    for i in (0, 1, 2, 3):
        for j in (1, 2, 3):
            ca[(i, j)].wait_recv()
            cb[(j, i)].wait_recv()
    for slot in range(8):
        ck[slot].wait_recv()

    factor = jnp.exp(jnp.full((1, 1), scale_ref[0], F32))
    offset = bias_ref[0]

    def tile(i):
        part = rows(pl.multiple_of(i * 128, 128), 128)
        logits = factor * lax.dot_general(
            txt[part, :], img[...], (((1,), (1,)), ((), ())), preferred_element_type=F32) + offset
        row = lax.broadcasted_iota(jnp.int32, (128, ALL), 0) + i * 128
        col = lax.broadcasted_iota(jnp.int32, (128, ALL), 1)
        want = jnp.where(row < HALF, row, row + 240)
        matched = jnp.where((row < ROWS) & (col == want), 1.0, 0.0).astype(F32)
        weights = (factor * (jax.nn.sigmoid(logits) - matched)).astype(BF16)
        wt[part, :] = weights
        tp[part, :] = jnp.dot(weights, img[...], preferred_element_type=F32).astype(BF16)

    pl.loop(2, 4)(tile)
    exchange = send(tp.at[rows(256, 256), :], tpd, s_k.at[8], r_k.at[8], at(dk=1))
    pl.loop(0, 2)(tile)
    exchange.wait_recv()

    def join(i):
        part = rows(pl.multiple_of(i * ROWS, ROWS), ROWS)
        tp[part, :] = (tp[part, :].astype(F32) + tpd[part, :].astype(F32)).astype(BF16)

    pl.loop(0, 8)(join)

    cr = {}

    def rz_slot(sign, dist, half):
        return ((0 if sign > 0 else 4) + dist - 1) * 2 + half

    def ship_rs(sign, dist, half):
        slot = dist if sign > 0 else (8 - dist)
        n = rz_slot(sign, dist, half)
        cr[(sign, dist, half)] = send(
            tp.at[rows(slot * ROWS + half * HALF, HALF), :], rz.at[n], s_rs.at[n], r_rs.at[n], at(dz=sign))

    def take_rs(sign, dist, half):
        cr[(sign, dist, half)].wait_recv()
        slot = (dist - 1) if sign > 0 else (9 - dist)
        part = rows(slot * ROWS + half * HALF, HALF)
        tp[part, :] = (tp[part, :].astype(F32) + rz[rz_slot(sign, dist, half)].astype(F32)).astype(BF16)
        ship_rs(sign, dist - 1, half)

    ship_rs(1, 4, 0)
    ship_rs(-1, 4, 1)
    ship_rs(1, 3, 1)
    ship_rs(-1, 3, 0)

    def image_tile(i):
        part = rows(pl.multiple_of(i * 128, 128), 128)
        ip[part, :] = lax.dot_general(
            wt[:, part], txt[...], (((0,), (0,)), ((), ())), preferred_element_type=F32).astype(BF16)

    ci = {}

    def ship_ir(name, dist, src, dst, n, where):
        ci[(name, dist)] = send(src, dst, s_ir.at[n], r_ir.at[n], where)

    pl.loop(0, 2)(image_tile)
    for i in order:
        ship_ir("ay", i, ip.at[rows(i * 64, 64), :], iay.at[i - 1], i - 1, at(dy=i))
    take_rs(1, 4, 0)
    take_rs(-1, 4, 1)
    take_rs(1, 3, 1)
    take_rs(-1, 3, 0)
    pl.loop(2, 4)(image_tile)
    for i in order:
        ship_ir("bx", i, ip.at[rows(256 + i * 64, 64), :], ibx.at[i - 1], 3 + i - 1, at(dx=i))
    take_rs(1, 3, 0)
    take_rs(-1, 3, 1)
    take_rs(1, 2, 1)
    take_rs(-1, 2, 0)

    def fold(base, recv, name):
        for i in order:
            ci[(name, i)].wait_recv()
        for j in range(4):
            part = rows(base + j * HALF, HALF)
            inner = rows(j * HALF, HALF)
            total = ip[part, :].astype(F32)
            for i in range(3):
                total = total + recv[i, inner, :].astype(F32)
            ip[part, :] = total.astype(BF16)

    fold(0, iay, "ay")
    for i in order:
        ship_ir("ax", i, ip.at[rows(i * HALF, HALF), :], iax.at[i - 1], 6 + i - 1, at(dx=i))
    take_rs(1, 2, 0)
    take_rs(-1, 2, 1)
    fold(256, ibx, "bx")
    for i in order:
        ship_ir("by", i, ip.at[rows(256 + i * HALF, HALF), :], iby.at[i - 1], 9 + i - 1, at(dy=i))

    for sign in (1, -1):
        for half in range(2):
            cr[(sign, 1, half)].wait_recv()
    halves = []
    for half in range(2):
        total = tp[rows(half * HALF, HALF), :].astype(F32)
        total = total + rz[rz_slot(1, 1, half)].astype(F32) + rz[rz_slot(-1, 1, half)].astype(F32)
        halves.append(total)
    text_sum = jnp.concatenate(halves, axis=0)
    text_dir = tdir[...]
    proj_grad = (
        (text_sum - text_dir * jnp.sum(text_dir * text_sum, axis=-1, keepdims=True)) / text_len
    ).astype(BF16)
    pall[0] = proj_grad

    cp = {}
    for dx in order:
        slot = 4 - dx
        cp[slot] = send(pall.at[0], pall.at[slot], s_p.at[slot], r_p.at[slot], at(dx=dx))
    cp[4] = send(pall.at[0], pall.at[4], s_p.at[4], r_p.at[4], at(dk=1))

    gt_ref[...] = lax.dot_general(
        proj_grad, head[...], (((1,), (1,)), ((), ())), preferred_element_type=F32).astype(BF16)

    for slot in (1, 3, 2):
        cp[slot].wait_recv()
        cp[4 + slot] = send(pall.at[slot], pall.at[4 + slot], s_p.at[4 + slot], r_p.at[4 + slot], at(dk=1))
    for slot in range(4, 8):
        cp[slot].wait_recv()
    for slot in range(1, 8):
        cf[slot].wait_recv()

    hp[...] = lax.dot_general(
        fall[...].reshape(256, COLS), pall[...].reshape(256, D), (((0,), (0,)), ((), ())),
        preferred_element_type=F32)
    for s in range(NZ):
        part = hp[rows(s * SLICE, SLICE), :]
        hm[s] = part[:HALF].astype(BF16)
        hl[s] = part[HALF:].astype(BF16)
    ch = {}
    for dz in (1, 7, 2, 6, 3, 5, 4):
        dest = (z + dz) % NZ
        ch[dz] = (
            send(hm.at[dest], rm.at[dz], s_h.at[dz], r_h.at[dz], at(dz=dz)),
            send(hl.at[dest], rl.at[dz], s_h.at[8 + dz], r_h.at[8 + dz], at(dz=dz)),
        )

    for name in ("ax", "by"):
        for i in order:
            ci[(name, i)].wait_recv()
    total_a = ip[rows(0, HALF), :].astype(F32)
    total_b = ip[rows(256, HALF), :].astype(F32)
    for i in range(3):
        total_a = total_a + iax[i].astype(F32)
        total_b = total_b + iby[i].astype(F32)
    image_sum = jnp.concatenate([total_a, total_b], axis=0)
    wide = image_ref[...].astype(F32)
    image_len = jnp.sqrt(jnp.sum(wide * wide, axis=-1, keepdims=True) + EPSILON)
    image_dir = wide / image_len
    gi_ref[...] = (
        (image_sum - image_dir * jnp.sum(image_dir * image_sum, axis=-1, keepdims=True)) / image_len
    ).astype(BF16)

    main = hm[z].astype(F32)
    left = hl[z].astype(F32)
    for dz in (1, 7, 2, 6, 3, 5, 4):
        for copy in ch[dz]:
            copy.wait_recv()
        main = main + rm[dz].astype(F32)
        left = left + rl[dz].astype(F32)
    sm[...] = main.astype(BF16)
    sl[...] = left.astype(BF16)

    y_lo = y % 2

    def final(target_y, target_k, slot):
        return (
            pltpu.make_async_remote_copy(
                src_ref=sm, dst_ref=qm.at[slot], send_sem=s_q.at[target_y // 2 * 2 + target_k],
                recv_sem=r_q.at[slot], device_id=device(x, target_y, z, target_k), device_id_type=MESH),
            pltpu.make_async_remote_copy(
                src_ref=sl, dst_ref=ql.at[slot], send_sem=s_q.at[4 + target_y // 2 * 2 + target_k],
                recv_sem=r_q.at[4 + slot], device_id=device(x, target_y, z, target_k), device_id_type=MESH),
        )

    for h in range(2):
        for tk in range(2):
            ty = k + 2 * h
            own = (ty == y) & (tk == k)

            @pl.when(jnp.logical_not(own))
            def _():
                for copy in final(ty, tk, y):
                    copy.start()

            @pl.when(own)
            def _():
                qm[y] = sm[...]
                ql[y] = sl[...]

    for sy in range(4):
        @pl.when(jnp.logical_not((sy == y) & (k == y_lo)))
        def _():
            for copy in final(y, k, sy):
                copy.wait_recv()

    main = qm[0].astype(F32)
    left = ql[0].astype(F32)
    for sy in range(1, 4):
        main = main + qm[sy].astype(F32)
        left = left + ql[sy].astype(F32)
    gh_ref[pl.ds(0, HALF), :] = main
    gh_ref[pl.ds(HALF, 2), :] = left

    for copy in sent:
        copy.wait_send()
    for h in range(2):
        for tk in range(2):
            ty = k + 2 * h

            @pl.when(jnp.logical_not((ty == y) & (tk == k)))
            def _():
                for copy in final(ty, tk, y):
                    copy.wait_send()


def local(image_embed, text_feature, text_head, log_scale, bias):
    fsel = text_feature.reshape(ROWS, NZ, 8, SLICE).transpose(2, 0, 1, 3).reshape(8, ROWS, COLS)
    vmem = pl.BlockSpec(memory_space=pltpu.VMEM)
    smem = pl.BlockSpec(memory_space=pltpu.SMEM)
    dma = pltpu.SemaphoreType.DMA
    V = pltpu.VMEM
    return pl.pallas_call(
        kernel,
        out_shape=(
            jax.ShapeDtypeStruct((ROWS, D), BF16),
            jax.ShapeDtypeStruct((ROWS, D), BF16),
            jax.ShapeDtypeStruct((SLICE, D), F32),
        ),
        in_specs=[smem, smem, vmem, vmem, vmem, pl.BlockSpec(memory_space=pl.ANY)],
        out_specs=(vmem, vmem, vmem),
        scratch_shapes=[
            V((D, D), BF16),
            V((ALL, D), BF16),
            V((ALL, D), BF16),
            V((ALL, ALL), BF16),
            V((ALL, D), BF16),
            V((ALL, D), BF16),
            V((256, D), BF16),
            V((16, HALF, D), BF16),
            V((3, 64, D), BF16),
            V((3, HALF, D), BF16),
            V((3, 64, D), BF16),
            V((3, HALF, D), BF16),
            V((ROWS, D), F32),
            V((8, ROWS, D), BF16),
            V((8, ROWS, COLS), BF16),
            V((COLS, D), F32),
            V((NZ, HALF, D), BF16),
            V((NZ, 2, D), BF16),
            V((NZ, HALF, D), BF16),
            V((NZ, 2, D), BF16),
            V((HALF, D), BF16),
            V((2, D), BF16),
            V((4, HALF, D), BF16),
            V((4, 2, D), BF16),
            dma,
            dma((32,)), dma((32,)),
            dma((16,)), dma((16,)),
            dma((9,)), dma((9,)),
            dma((8,)), dma((8,)),
            dma((16,)), dma((16,)),
            dma((12,)), dma((12,)),
            dma((8,)), dma((8,)),
            dma((16,)), dma((16,)),
            dma((8,)), dma((8,)),
        ],
        compiler_params=pltpu.CompilerParams(
            collective_id=0, has_side_effects=True, vmem_limit_bytes=48 * 2**20),
        name="contrastive",
    )(log_scale, bias, image_embed, text_feature, fsel, text_head)


def solution(mesh):
    both = P(("grp", "blk"), None)
    return jax.shard_map(
        local,
        mesh=mesh,
        in_specs=(both, both, P(), P(), P()),
        out_specs=(both, both, P("blk", None)),
        check_vma=False,
    )
```

time: 348 us -> 78.2 us (0.22)
  waiting for transfers between devices: 244 us -> 0 us
  Pallas kernels: 0 us -> 67.4 us
  starting transfers between devices: 34.5 us -> 0 us
  matrix products: 16 us -> 0 us
  local copies, waits for them, and re-layouts: 23.6 us -> 8.54 us
  between operations: 15.2 us -> 1.97 us
  other arithmetic: 8.45 us -> 0 us
  blocking collectives: 4.61 us -> 0 us
    reduce_scatter x3 -> x0, waiting for transfers between devices: 104 us -> none  [own_block(): parts = lax.psum_scatter(parts, axes[k], scatter_dimension=0, tiled=True)]
    all_gather x2 -> x0, waiting for transfers between devices: 85.2 us -> none  [all_blocks(): parts = lax.all_gather(parts, axes[k])]
    pallas_call x0 -> x1, Pallas kernels: none -> 67.4 us  [local(): pl.pallas_call(kernel, out_shape=(jax.ShapeDtypeStruct((ROWS, D), BF16),...]
    all_to_all x5 -> x0, waiting for transfers between devices: 55 us -> none  [the longest x2 29.2 us: sent_and_summed(): parts = lax.all_to_all(cut_along(value, dim, peers), axis, 0, 0, tiled=True)]
    all_to_all x5 -> x0, starting transfers between devices: 34.4 us -> none  [the longest x2 17.2 us: sent_to_all(): lax.all_to_all(jnp.broadcast_to(value[None], (peers, *value.shape)), axis...]
    dot_general x6 -> x0, matrix products: 16 us -> none  [the longest x1 4.16 us: local(): lax.dot_general(gathered, text_all, (((1,), (1,)), ((), ())), preferred_e...]
    transpose x2 -> x1, local copies, waits for them, and re-layouts: 9.46 us -> 0.79 us  [local(): text_feature.reshape(ROWS, NZ, 8, SLICE).transpose(2, 0, 1, 3)]
    another operation x2 -> x0, local copies, waits for them, and re-layouts: 8.11 us -> none  [the longest x1 5.31 us: cut_along(): value.reshape(*dims[:dim], peers, dims[dim] // peers, *dims[dim + 1:])]
  transfers between devices with their start and end apart: 10 -> 0, of which waited for: 9 -> 0; matrix products, arithmetic and copies ran while one was open for 5% -> 0% of each run, Pallas kernels for 0% -> 0%
where the time goes in v1:
time: 78.2 us; the launch traced here: 78 us
  Pallas kernels  67.4 us (86%)
  local copies, waits for them, and re-layouts  8.54 us (11%)
  between operations  1.97 us (3%)
    pallas_call x1, Pallas kernels, local(): pl.pallas_call(kernel, out_shape=(jax.ShapeDtypeStruct((ROWS, D), BF16),...  67.4 us
    unnamed x9, local copies, waits for them, and re-layouts  5.42 us
    reshape x2, local copies, waits for them, and re-layouts, local(): text_feature.reshape(ROWS, NZ, 8, SLICE).transpose(2, 0, 1, 3)  2.33 us

profile of v1, /device:TPU:1, one launch (start us, length us, event | category | flops | bytes accessed | tf_op | source)
XLA Modules:
  0.0 78.0 jit_solution(10993021156317750210)
XLA Ops:
  0.6 2.1 %reshape.12 = bf16[32,8,8,18]{3,2,1,0:T(8,128)(2,1)S(1)} reshape(bf16[32,1152]{1,0:T(8,128)(2,1)} %text_ref.1) | data formatting | bytes 147456 | tf_op jit(solution)/shard_map/reshape | solution.py:402
  2.7 0.8 %copy.9 = bf16[8,32,8,18]{1,0,3,2:T(8,128)(2,1)S(1)} copy(bf16[8,32,8,18]{3,0,2,1:T(8,128)(2,1)S(1)} %bitcast.2) | data formatting | bytes 147456 | tf_op jit(solution)/shard_map/transpose | solution.py:402
  3.5 0.2 copy.10.fsel_ref
  5.1 0.0 copy-start
  5.1 1.7 %copy-done = bf16[1152,1152]{1,0:T(8,128)(2,1)S(1)} copy-done((bf16[1152,1152]{1,0:T(8,128)(2,1)S(1)}, bf16[1152,1152]{1,0:T(8,128)(2,1)}, u32[]{:S(2)}) %copy-start) | copy-done | bytes 2654232
  6.8 0.0 copy-start.1
  6.8 0.9 %copy-done.1 = bf16[32,1152]{1,0:T(8,128)(2,1)S(1)} copy-done((bf16[32,1152]{1,0:T(8,128)(2,1)S(1)}, bf16[32,1152]{1,0:T(8,128)(2,1)}, u32[]{:S(2)}) %copy-start.1) | copy-done | bytes 73752
  7.7 0.0 copy-start.2
  7.7 0.9 %copy-done.2 = bf16[32,1152]{1,0:T(8,128)(2,1)S(1)} copy-done((bf16[32,1152]{1,0:T(8,128)(2,1)S(1)}, bf16[32,1152]{1,0:T(8,128)(2,1)}, u32[]{:S(2)}) %copy-start.2) | copy-done | bytes 73752
  8.6 67.4 %contrastive.1 = (bf16[32,1152]{1,0:T(8,128)(2,1)S(1)}, bf16[32,1152]{1,0:T(8,128)(2,1)S(1)}, f32[18,1152]{1,0:T(8,128)S(1)}) custom-call(f32[1]{0:T(128)S(6)} %copy.14.scale_ref, f32[1]{0:T(128)S(6)} %copy.15.bias_ref, bf16[32,1152]{1,0:T(8,128)(2,1)S(1)} %copy-done.2, bf16[32,1152]{1,0:T(8,128)(2,1)S(1)} %copy-done.1, ...), custom_call_target="tpu_custom_call" | custom-call | tf_op jit(solution)/shard_map/contrastive/pallas_call | solution.py:407
  76.0 0.6 copy.16
  76.7 0.6 copy.17
  77.3 0.6 copy.18
Async XLA Ops:
  5.1 1.8 %copy-start = (bf16[1152,1152]{1,0:T(8,128)(2,1)S(1)}, bf16[1152,1152]{1,0:T(8,128)(2,1)}, u32[]{:S(2)}) copy-start(bf16[1152,1152]{1,0:T(8,128)(2,1)} %head_hbm.1) | copy-start | bytes 7962628
  6.8 0.9 %copy-start.1 = (bf16[32,1152]{1,0:T(8,128)(2,1)S(1)}, bf16[32,1152]{1,0:T(8,128)(2,1)}, u32[]{:S(2)}) copy-start(bf16[32,1152]{1,0:T(8,128)(2,1)} %text_ref.1) | copy-start | bytes 221188
  7.7 0.9 %copy-start.2 = (bf16[32,1152]{1,0:T(8,128)(2,1)S(1)}, bf16[32,1152]{1,0:T(8,128)(2,1)}, u32[]{:S(2)}) copy-start(bf16[32,1152]{1,0:T(8,128)(2,1)} %image_ref.1) | copy-start | bytes 221188

commit v2 on v1

v2 whole, which is shorter than its diff:
```python
import jax
import jax.numpy as jnp
from jax import lax
from jax.experimental import pallas as pl
from jax.experimental.pallas import tpu as pltpu
from jax.sharding import PartitionSpec as P

MESH = pl.DeviceIdType.MESH
EPSILON = 1e-06
F32 = jnp.float32
BF16 = jnp.bfloat16
D = 1152
ROWS = 32
HALF = 16
NX, NY, NZ, NK = 4, 4, 8, 2
ALL = 512
COLS = D // NZ
SLICE = 18


def place():
    grp = lax.axis_index("grp")
    blk = lax.axis_index("blk")
    return blk % 4, (grp // 2) * 2 + (blk // 4) % 2, blk // 8, grp % 2


def device(x, y, z, k):
    return ((y // 2) * 2 + k, z * 8 + (y % 2) * 4 + x)


GROUPS = ((0, 1), (2, 7), (3, 6), (4, 5))
TEXT_ROW = {s: g * 128 + j * ROWS for g, pair in enumerate(GROUPS) for j, s in enumerate(pair)}
CHUNKS = ((0, 640), (640, 512))


def rows(start, count):
    return pl.ds(start, count)


def kernel(
    scalar_ref, image_hbm, text_hbm, head_hbm,
    gi_hbm, gt_hbm, gh_hbm,
    gi_ref, gt_ref, gh_ref, image_ref, text_ref, fsel_ref, head, img, txt, wt, tp, ip, tpd, rz, iay, iax, ibx, iby,
    tdir, pall, fall, hp, hm, hl, rm, rl, sm, sl, qm, ql,
    in_sem, out_sem, s_img, r_img, s_z, r_z, s_k, r_k, s_f, r_f, s_rs, r_rs, s_ir, r_ir,
    s_p, r_p, s_h, r_h, s_q, r_q,
):
    x, y, z, k = place()

    def at(dx=0, dy=0, dz=0, dk=0):
        return device((x + dx) % NX, (y + dy) % NY, (z + dz) % NZ, (k + dk) % NK)

    sent = []

    def send(src, dst, ssem, rsem, where):
        copy = pltpu.make_async_remote_copy(
            src_ref=src, dst_ref=dst, send_sem=ssem, recv_sem=rsem,
            device_id=where, device_id_type=MESH,
        )
        copy.start()
        sent.append(copy)
        return copy

    loads = []
    for n, (src, dst) in enumerate((
        (image_hbm, image_ref), (head_hbm, head), (text_hbm, text_ref),
    )):
        loads.append(pltpu.make_async_copy(src, dst, in_sem.at[n]))
        loads[n].start()

    barrier = pltpu.get_barrier_semaphore()
    partners = (
        [dict(dx=i) for i in (1, 2, 3)]
        + [dict(dy=i) for i in (1, 2, 3)]
        + [dict(dz=1), dict(dz=7), dict(dk=1)]
    )
    for p in partners:
        pl.semaphore_signal(barrier, inc=1, device_id=at(**p), device_id_type=MESH)

    loads[0].wait()
    wide = image_ref[...].astype(F32)
    image_len = jnp.sqrt(jnp.sum(wide * wide, axis=-1, keepdims=True) + EPSILON)
    low = (wide / image_len).astype(BF16)
    img[rows(0, HALF), :] = low[:HALF]
    img[rows(256, HALF), :] = low[HALF:]

    pl.semaphore_wait(barrier, len(partners))

    ca, cb = {}, {}

    def send_a(dx, dy, sx):
        src = img.at[rows(sx * HALF, HALF), :]
        tx, ty = dx, dy
        slot = ty * 4 + tx
        return src, img.at[rows(slot * HALF, HALF), :], slot

    def ship_a(tx, ty, sx, where):
        src = img.at[rows(sx * HALF, HALF), :]
        slot = ty * 4 + tx
        ca[(tx, ty)] = send(src, img.at[rows(slot * HALF, HALF), :],
                            s_img.at[slot], r_img.at[slot], where)

    def ship_b(tx, ty, sy, where):
        src = img.at[rows(256 + sy * HALF, HALF), :]
        slot = tx * 4 + ty
        cb[(tx, ty)] = send(src, img.at[rows(256 + slot * HALF, HALF), :],
                            s_img.at[16 + slot], r_img.at[16 + slot], where)

    order = (1, 3, 2)
    for i in order:
        ship_a(4 - i, 0, 0, at(dx=i))
        ship_b(0, 4 - i, 0, at(dy=i))
    for i in order:
        ship_a(0, 4 - i, 0, at(dy=i))
        ship_b(4 - i, 0, 0, at(dx=i))

    loads[1].wait()
    loads[2].wait()
    projected = jnp.dot(text_ref[...], head[...], preferred_element_type=F32)
    text_len = jnp.sqrt(jnp.sum(projected * projected, axis=-1, keepdims=True) + EPSILON)
    text_dir = projected / text_len
    tdir[...] = text_dir
    txt[rows(0, ROWS), :] = text_dir.astype(BF16)

    cz = {}

    def ship_zc(sign, step, half, c):
        src_slot = ((8 - (step - 1)) % 8) if sign > 0 else step - 1
        dst_slot = (8 - step) if sign > 0 else step
        n = (((0 if sign > 0 else 4) + step - 1) * 2 + half) * 2 + c
        cz[(sign, step, half, c)] = send(
            txt.at[rows(TEXT_ROW[src_slot] + half * HALF, HALF), pl.ds(*CHUNKS[c])],
            txt.at[rows(TEXT_ROW[dst_slot] + half * HALF, HALF), pl.ds(*CHUNKS[c])],
            s_z.at[n], r_z.at[n], at(dz=sign))

    ck = {}

    def ship_k(slot):
        ck[slot] = send(txt.at[rows(TEXT_ROW[slot], ROWS), :], txt.at[rows(TEXT_ROW[slot] + 64, ROWS), :],
                        s_k.at[slot], r_k.at[slot], at(dk=1))

    for half in range(2):
        for c in range(2):
            ship_zc(1, 1, half, c)
            ship_zc(-1, 1, half, c)
    ship_k(0)

    def forward_image(i):
        ca[(i, 0)].wait_recv()
        for j in order:
            ship_a(i, 4 - j, i, at(dy=j))
        cb[(0, i)].wait_recv()
        for j in order:
            ship_b(4 - j, i, i, at(dx=j))

    column = lax.broadcasted_iota(jnp.int32, (1, COLS), 1)
    source = column
    for n in range(1, NZ):
        source = source + jnp.where(column >= n * SLICE, COLS - SLICE, 0)
    entry = lax.broadcasted_iota(jnp.int32, (D, COLS), 0)

    def select(q):
        chosen = jnp.where(entry == source + q * SLICE, 1.0, 0.0).astype(BF16)
        fsel_ref[q] = jnp.dot(text_ref[...], chosen, preferred_element_type=F32).astype(BF16)

    forward_image(3)
    forward_image(1)
    for step in (1, 2, 3):
        for half in range(2):
            for c in range(2):
                cz[(1, step, half, c)].wait_recv()
                if step < 3 or half == 0:
                    ship_zc(1, step + 1, half, c)
                cz[(-1, step, half, c)].wait_recv()
                if step < 3 or half == 1:
                    ship_zc(-1, step + 1, half, c)
        ship_k(8 - step)
        ship_k(step)
        if step == 1:
            forward_image(2)
            pl.loop(0, 4)(select)
        if step == 2:
            pl.loop(4, 8)(select)
    for c in range(2):
        cz[(1, 4, 0, c)].wait_recv()
        cz[(-1, 4, 1, c)].wait_recv()
    ship_k(4)

    for i in (0, 1, 2, 3):
        for j in (1, 2, 3):
            ca[(i, j)].wait_recv()
            cb[(j, i)].wait_recv()
    for slot in range(8):
        ck[slot].wait_recv()

    factor = jnp.exp(jnp.full((1, 1), scalar_ref[0], F32))
    offset = scalar_ref[1]

    def tile(i):
        part = rows(i * 128, 128)
        logits = factor * lax.dot_general(
            txt[part, :], img[...], (((1,), (1,)), ((), ())), preferred_element_type=F32) + offset
        prob = jax.nn.sigmoid(logits)
        if i == 0:
            row = lax.broadcasted_iota(jnp.int32, (128, ALL), 0)
            col = lax.broadcasted_iota(jnp.int32, (128, ALL), 1)
            want = jnp.where(row < HALF, row, row + 240)
            prob = prob - jnp.where((row < ROWS) & (col == want), 1.0, 0.0).astype(F32)
        weights = (factor * prob).astype(BF16)
        wt[part, :] = weights
        tp[part, :] = jnp.dot(weights, img[...], preferred_element_type=F32).astype(BF16)

    ce = {}

    def give(g):
        tile(g)
        ce[g] = send(tp.at[rows(g * 128 + 64, 64), :], tpd.at[g], s_k.at[8 + g], r_k.at[8 + g], at(dk=1))

    def join(g):
        ce[g].wait_recv()
        for j in range(4):
            part = rows(g * 128 + j * HALF, HALF)
            tp[part, :] = (tp[part, :].astype(F32) + tpd[g, rows(j * HALF, HALF), :].astype(F32)).astype(BF16)

    cr = {}

    def rz_slot(sign, dist, half):
        return ((0 if sign > 0 else 4) + dist - 1) * 2 + half

    def ship_rs(sign, dist, half, c):
        slot = dist if sign > 0 else (8 - dist)
        n = rz_slot(sign, dist, half)
        cols = pl.ds(*CHUNKS[c])
        cr[(sign, dist, half, c)] = send(
            tp.at[rows(TEXT_ROW[slot] + half * HALF, HALF), cols], rz.at[n, :, cols],
            s_rs.at[n * 2 + c], r_rs.at[n * 2 + c], at(dz=sign))

    def take_rs(sign, dist, half):
        slot = (dist - 1) if sign > 0 else (9 - dist)
        part = rows(TEXT_ROW[slot] + half * HALF, HALF)
        for c in range(2):
            cols = pl.ds(*CHUNKS[c])
            cr[(sign, dist, half, c)].wait_recv()
            tp[part, cols] = (
                tp[part, cols].astype(F32) + rz[rz_slot(sign, dist, half), :, cols].astype(F32)
            ).astype(BF16)
            ship_rs(sign, dist - 1, half, c)

    def image_tile(i):
        part = rows(i * 128, 128)
        ip[part, :] = lax.dot_general(
            wt[:, part], txt[...], (((0,), (0,)), ((), ())), preferred_element_type=F32).astype(BF16)

    ci = {}

    def ship_ir(name, dist, src, dst, n, where):
        ci[(name, dist)] = send(src, dst, s_ir.at[n], r_ir.at[n], where)

    give(3)
    give(2)
    join(3)
    for c in range(2):
        ship_rs(1, 4, 0, c)
        ship_rs(-1, 4, 1, c)
        ship_rs(-1, 3, 0, c)
    join(2)
    for c in range(2):
        ship_rs(1, 3, 1, c)
    give(1)
    give(0)
    join(1)
    take_rs(1, 4, 0)
    take_rs(-1, 4, 1)
    take_rs(1, 3, 1)
    take_rs(-1, 3, 0)
    join(0)

    fall[0] = fsel_ref[k * 4 + x]
    cf = {}
    for dk in range(2):
        for dx in range(4):
            if dk == 0 and dx == 0:
                continue
            slot = ((4 - dx) % 4) + 4 * dk
            cf[slot] = send(fsel_ref.at[((k + dk) % 2) * 4 + (x + dx) % 4], fall.at[slot],
                            s_f.at[slot], r_f.at[slot], at(dx=dx, dk=dk))

    image_tile(0)
    image_tile(1)
    for i in order:
        ship_ir("ay", i, ip.at[rows(i * 64, 64), :], iay.at[i - 1], i - 1, at(dy=i))
    take_rs(1, 3, 0)
    take_rs(-1, 3, 1)
    take_rs(1, 2, 1)
    take_rs(-1, 2, 0)
    image_tile(2)
    image_tile(3)
    for i in order:
        ship_ir("bx", i, ip.at[rows(256 + i * 64, 64), :], ibx.at[i - 1], 3 + i - 1, at(dx=i))

    def fold(base, recv, name):
        for i in order:
            ci[(name, i)].wait_recv()
        for j in range(4):
            part = rows(base + j * HALF, HALF)
            inner = rows(j * HALF, HALF)
            total = ip[part, :].astype(F32)
            for i in range(3):
                total = total + recv[i, inner, :].astype(F32)
            ip[part, :] = total.astype(BF16)

    take_rs(1, 2, 0)
    take_rs(-1, 2, 1)

    for half in range(2):
        for sign in (1, -1):
            for c in range(2):
                cr[(sign, 1, half, c)].wait_recv()
    halves = []
    for half in range(2):
        total = tp[rows(half * HALF, HALF), :].astype(F32)
        total = total + rz[rz_slot(1, 1, half)].astype(F32) + rz[rz_slot(-1, 1, half)].astype(F32)
        halves.append(total)
    text_sum = jnp.concatenate(halves, axis=0)
    text_dir = tdir[...]
    proj_grad = (
        (text_sum - text_dir * jnp.sum(text_dir * text_sum, axis=-1, keepdims=True)) / text_len
    ).astype(BF16)
    pall[0] = proj_grad

    cp = {}
    for dx in order:
        slot = 4 - dx
        cp[slot] = send(pall.at[0], pall.at[slot], s_p.at[slot], r_p.at[slot], at(dx=dx))
    cp[4] = send(pall.at[0], pall.at[4], s_p.at[4], r_p.at[4], at(dk=1))

    gt_ref[...] = lax.dot_general(
        proj_grad, head[...], (((1,), (1,)), ((), ())), preferred_element_type=F32).astype(BF16)

    outs = [
        pltpu.make_async_copy(src, dst, out_sem.at[n])
        for n, (src, dst) in enumerate(((gi_ref, gi_hbm), (gt_ref, gt_hbm), (gh_ref, gh_hbm)))
    ]
    outs[1].start()
    fold(0, iay, "ay")
    for i in order:
        ship_ir("ax", i, ip.at[rows(i * HALF, HALF), :], iax.at[i - 1], 6 + i - 1, at(dx=i))
    fold(256, ibx, "bx")
    for i in order:
        ship_ir("by", i, ip.at[rows(256 + i * HALF, HALF), :], iby.at[i - 1], 9 + i - 1, at(dy=i))

    for slot in (1, 3, 2):
        cp[slot].wait_recv()
        cp[4 + slot] = send(pall.at[slot], pall.at[4 + slot], s_p.at[4 + slot], r_p.at[4 + slot], at(dk=1))
    for slot in range(4, 8):
        cp[slot].wait_recv()
    for slot in range(1, 8):
        cf[slot].wait_recv()

    hp[...] = lax.dot_general(
        fall[...].reshape(256, COLS), pall[...].reshape(256, D), (((0,), (0,)), ((), ())),
        preferred_element_type=F32)
    for s in range(NZ):
        part = hp[rows(s * SLICE, SLICE), :]
        hm[s] = part[:HALF].astype(BF16)
        hl[s] = part[HALF:].astype(BF16)
    ch = {}
    for dz in (1, 7, 2, 6, 3, 5, 4):
        dest = (z + dz) % NZ
        ch[dz] = (
            send(hm.at[dest], rm.at[dz], s_h.at[dz], r_h.at[dz], at(dz=dz)),
            send(hl.at[dest], rl.at[dz], s_h.at[8 + dz], r_h.at[8 + dz], at(dz=dz)),
        )

    for name in ("ax", "by"):
        for i in order:
            ci[(name, i)].wait_recv()
    total_a = ip[rows(0, HALF), :].astype(F32)
    total_b = ip[rows(256, HALF), :].astype(F32)
    for i in range(3):
        total_a = total_a + iax[i].astype(F32)
        total_b = total_b + iby[i].astype(F32)
    image_sum = jnp.concatenate([total_a, total_b], axis=0)
    wide = image_ref[...].astype(F32)
    image_len = jnp.sqrt(jnp.sum(wide * wide, axis=-1, keepdims=True) + EPSILON)
    image_dir = wide / image_len
    gi_ref[...] = (
        (image_sum - image_dir * jnp.sum(image_dir * image_sum, axis=-1, keepdims=True)) / image_len
    ).astype(BF16)

    outs[0].start()
    main = hm[z].astype(F32)
    left = hl[z].astype(F32)
    for dz in (1, 7, 2, 6, 3, 5, 4):
        for copy in ch[dz]:
            copy.wait_recv()
        main = main + rm[dz].astype(F32)
        left = left + rl[dz].astype(F32)
    sm[...] = main.astype(BF16)
    sl[...] = left.astype(BF16)

    y_lo = y % 2

    def final(target_y, target_k, slot):
        return (
            pltpu.make_async_remote_copy(
                src_ref=sm, dst_ref=qm.at[slot], send_sem=s_q.at[target_y // 2 * 2 + target_k],
                recv_sem=r_q.at[slot], device_id=device(x, target_y, z, target_k), device_id_type=MESH),
            pltpu.make_async_remote_copy(
                src_ref=sl, dst_ref=ql.at[slot], send_sem=s_q.at[4 + target_y // 2 * 2 + target_k],
                recv_sem=r_q.at[4 + slot], device_id=device(x, target_y, z, target_k), device_id_type=MESH),
        )

    for h in range(2):
        for tk in range(2):
            ty = k + 2 * h
            own = (ty == y) & (tk == k)

            @pl.when(jnp.logical_not(own))
            def _():
                for copy in final(ty, tk, y):
                    copy.start()

            @pl.when(own)
            def _():
                qm[y] = sm[...]
                ql[y] = sl[...]

    for sy in range(4):
        @pl.when(jnp.logical_not((sy == y) & (k == y_lo)))
        def _():
            for copy in final(y, k, sy):
                copy.wait_recv()

    main = qm[0].astype(F32)
    left = ql[0].astype(F32)
    for sy in range(1, 4):
        main = main + qm[sy].astype(F32)
        left = left + ql[sy].astype(F32)
    gh_ref[pl.ds(0, HALF), :] = main
    gh_ref[pl.ds(HALF, 2), :] = left
    outs[2].start()

    for copy in sent:
        copy.wait_send()
    for h in range(2):
        for tk in range(2):
            ty = k + 2 * h

            @pl.when(jnp.logical_not((ty == y) & (tk == k)))
            def _():
                for copy in final(ty, tk, y):
                    copy.wait_send()
    for copy in outs:
        copy.wait()


def deliver(gi_in, gt_in, gh_in, gi_out, gt_out, gh_out, gi_ref, gt_ref, gh_ref, in_sem, out_sem):
    first = [
        pltpu.make_async_copy(src, dst, in_sem.at[n])
        for n, (src, dst) in enumerate(((gi_in, gi_ref), (gt_in, gt_ref), (gh_in, gh_ref)))
    ]
    second = [
        pltpu.make_async_copy(src, dst, out_sem.at[n])
        for n, (src, dst) in enumerate(((gi_ref, gi_out), (gt_ref, gt_out), (gh_ref, gh_out)))
    ]
    for copy in first:
        copy.start()
    for n in range(3):
        first[n].wait()
        second[n].start()
    for copy in second:
        copy.wait()


def local(image_embed, text_feature, text_head, log_scale, bias):
    hbm = pl.BlockSpec(memory_space=pltpu.HBM)
    dma = pltpu.SemaphoreType.DMA
    V = pltpu.VMEM
    shapes = (
        jax.ShapeDtypeStruct((ROWS, D), BF16),
        jax.ShapeDtypeStruct((ROWS, D), BF16),
        jax.ShapeDtypeStruct((SLICE, D), F32),
    )
    results = pl.pallas_call(
        kernel,
        out_shape=shapes,
        in_specs=[pl.BlockSpec(memory_space=pltpu.SMEM)] + [hbm] * 3,
        out_specs=(hbm, hbm, hbm),
        scratch_shapes=[
            V((ROWS, D), BF16),
            V((ROWS, D), BF16),
            V((SLICE, D), F32),
            V((ROWS, D), BF16),
            V((ROWS, D), BF16),
            V((8, ROWS, COLS), BF16),
            V((D, D), BF16),
            V((ALL, D), BF16),
            V((ALL, D), BF16),
            V((ALL, ALL), BF16),
            V((ALL, D), BF16),
            V((ALL, D), BF16),
            V((4, 64, D), BF16),
            V((16, HALF, D), BF16),
            V((3, 64, D), BF16),
            V((3, HALF, D), BF16),
            V((3, 64, D), BF16),
            V((3, HALF, D), BF16),
            V((ROWS, D), F32),
            V((8, ROWS, D), BF16),
            V((8, ROWS, COLS), BF16),
            V((COLS, D), F32),
            V((NZ, HALF, D), BF16),
            V((NZ, 2, D), BF16),
            V((NZ, HALF, D), BF16),
            V((NZ, 2, D), BF16),
            V((HALF, D), BF16),
            V((2, D), BF16),
            V((4, HALF, D), BF16),
            V((4, 2, D), BF16),
            dma((3,)), dma((3,)),
            dma((32,)), dma((32,)),
            dma((32,)), dma((32,)),
            dma((12,)), dma((12,)),
            dma((8,)), dma((8,)),
            dma((32,)), dma((32,)),
            dma((12,)), dma((12,)),
            dma((8,)), dma((8,)),
            dma((16,)), dma((16,)),
            dma((8,)), dma((8,)),
        ],
        compiler_params=pltpu.CompilerParams(
            collective_id=0, has_side_effects=True, vmem_limit_bytes=66500000),
        name="contrastive",
    )(jnp.concatenate([log_scale, bias]), image_embed, text_feature, text_head)
    return pl.pallas_call(
        deliver,
        out_shape=shapes,
        in_specs=[hbm] * 3,
        out_specs=(hbm, hbm, hbm),
        scratch_shapes=[
            V((ROWS, D), BF16), V((ROWS, D), BF16), V((SLICE, D), F32), dma((3,)), dma((3,))],
        compiler_params=pltpu.CompilerParams(vmem_limit_bytes=66500000),
        name="deliver",
    )(*results)


def solution(mesh):
    both = P(("grp", "blk"), None)
    return jax.shard_map(
        local,
        mesh=mesh,
        in_specs=(both, both, P(), P(), P()),
        out_specs=(both, both, P("blk", None)),
        check_vma=False,
    )
```

time: 78.2 us -> 72 us (0.921)
  local copies, waits for them, and re-layouts: 8.54 us -> 0 us
  Pallas kernels: 67.4 us -> 69.3 us
    unnamed x9 -> x0, local copies, waits for them, and re-layouts: 5.42 us -> none
    reshape x2 -> x0, local copies, waits for them, and re-layouts: 2.33 us -> none  [local(): text_feature.reshape(ROWS, NZ, 8, SLICE).transpose(2, 0, 1, 3)]
    pallas_call x1 -> x2, Pallas kernels: 67.4 us -> 69.3 us  [the longest x1 67.6 us: local(): pl.pallas_call(kernel, out_shape=shapes, in_specs=[pl.BlockSpec(memory_sp...]
    transpose x1 -> x0, local copies, waits for them, and re-layouts: 0.79 us -> none  [local(): text_feature.reshape(ROWS, NZ, 8, SLICE).transpose(2, 0, 1, 3)]
where the time goes in v2:
time: 72 us; the launch traced here: 71.8 us
  Pallas kernels  69.3 us (96%)
  between operations  1.93 us (3%)
    pallas_call x1, Pallas kernels, local(): pl.pallas_call(kernel, out_shape=shapes, in_specs=[pl.BlockSpec(memory_sp...  67.6 us
    pallas_call x1, Pallas kernels, local(): pl.pallas_call(deliver, out_shape=shapes, in_specs=[hbm] * 3, out_specs=(...  1.66 us

profile of v2, /device:TPU:1, one launch (start us, length us, event | category | flops | bytes accessed | tf_op | source)
XLA Modules:
  0.0 71.8 jit_solution(6563848073885430660)
XLA Ops:
  1.9 0.6 pad_maximum_fusion.scalar_ref
  2.5 67.6 %contrastive.1 = (bf16[32,1152]{1,0:T(8,128)(2,1)}, bf16[32,1152]{1,0:T(8,128)(2,1)}, f32[18,1152]{1,0:T(8,128)}) custom-call(f32[2]{0:T(128)} %pad_maximum_fusion.scalar_ref, bf16[32,1152]{1,0:T(8,128)(2,1)} %image_hbm.1, bf16[32,1152]{1,0:T(8,128)(2,1)} %text_hbm.1, bf16[1152,1152]{1,0:T(8,128)(2,1)} %head_hbm.1), custom_call_target="tpu_custom_call" | custom-call | tf_op jit(solution)/shard_map/contrastive/pallas_call | solution.py:485
  70.1 1.7 %deliver.1 = (bf16[32,1152]{1,0:T(8,128)(2,1)}, bf16[32,1152]{1,0:T(8,128)(2,1)}, f32[18,1152]{1,0:T(8,128)}) custom-call(bf16[32,1152]{1,0:T(8,128)(2,1)} %get-tuple-element.6.gi_in, bf16[32,1152]{1,0:T(8,128)(2,1)} %get-tuple-element.7.gt_in, f32[18,1152]{1,0:T(8,128)} %get-tuple-element.8.gh_in), custom_call_target="tpu_custom_call" | custom-call | tf_op jit(solution)/shard_map/deliver/pallas_call | solution.py:536

commit v3 on v2

--- a/solution.py
+++ b/solution.py
@@ -13,7 +13,6 @@
 ROWS = 32
 HALF = 16
 NX, NY, NZ, NK = 4, 4, 8, 2
-ALL = 512
 COLS = D // NZ
 SLICE = 18
 
@@ -28,8 +27,9 @@
     return ((y // 2) * 2 + k, z * 8 + (y % 2) * 4 + x)
 
 
-GROUPS = ((0, 1), (2, 7), (3, 6), (4, 5))
-TEXT_ROW = {s: g * 128 + j * ROWS for g, pair in enumerate(GROUPS) for j, s in enumerate(pair)}
+TEXT_ROW = {s: n * ROWS for n, s in enumerate((0, 1, 7, 2, 6, 3, 5, 4))}
+TEXTS = 256
+IMAGES = 1024
 CHUNKS = ((0, 640), (640, 512))
 
 
@@ -40,26 +40,29 @@
 def kernel(
     scalar_ref, image_hbm, text_hbm, head_hbm,
     gi_hbm, gt_hbm, gh_hbm,
-    gi_ref, gt_ref, gh_ref, image_ref, text_ref, fsel_ref, head, img, txt, wt, tp, ip, tpd, rz, iay, iax, ibx, iby,
-    tdir, pall, fall, hp, hm, hl, rm, rl, sm, sl, qm, ql,
-    in_sem, out_sem, s_img, r_img, s_z, r_z, s_k, r_k, s_f, r_f, s_rs, r_rs, s_ir, r_ir,
-    s_p, r_p, s_h, r_h, s_q, r_q,
+    gi_ref, gt_ref, gh_ref, image_ref, text_ref, fsel_ref, head, img, txt, wt, tp, ip, rz, iay, iax, ibx, iby,
+    ipd, tdir, pall, fall, hp, hm, hl, rm, rl, sm, sl, qm, ql,
+    in_sem, out_sem, r_first, r_second, r_pair, r_z, r_f, r_rs, r_rs1, r_ex, r_ir,
+    r_p, r_pk, r_hm, r_hl, s_q, r_q, s_all,
 ):
     x, y, z, k = place()
 
     def at(dx=0, dy=0, dz=0, dk=0):
         return device((x + dx) % NX, (y + dy) % NY, (z + dz) % NZ, (k + dk) % NK)
 
-    sent = []
-
-    def send(src, dst, ssem, rsem, where):
+    def send(src, dst, group, rsem, where):
         copy = pltpu.make_async_remote_copy(
-            src_ref=src, dst_ref=dst, send_sem=ssem, recv_sem=rsem,
+            src_ref=src, dst_ref=dst, send_sem=s_all.at[group], recv_sem=rsem,
             device_id=where, device_id_type=MESH,
         )
         copy.start()
-        sent.append(copy)
         return copy
+
+    def wait_all(ref, sem):
+        pltpu.make_async_remote_copy(
+            src_ref=ref, dst_ref=ref, send_sem=sem, recv_sem=sem,
+            device_id=at(dk=1), device_id_type=MESH,
+        ).wait_recv()
 
     loads = []
     for n, (src, dst) in enumerate((
@@ -88,23 +91,23 @@
 
     ca, cb = {}, {}
 
-    def send_a(dx, dy, sx):
-        src = img.at[rows(sx * HALF, HALF), :]
-        tx, ty = dx, dy
-        slot = ty * 4 + tx
-        return src, img.at[rows(slot * HALF, HALF), :], slot
+    def sem_of(first, i, j):
+        return r_first.at[first * 3 + i - 1] if j == 0 else r_second.at[first * 3 + j - 1]
 
     def ship_a(tx, ty, sx, where):
-        src = img.at[rows(sx * HALF, HALF), :]
-        slot = ty * 4 + tx
-        ca[(tx, ty)] = send(src, img.at[rows(slot * HALF, HALF), :],
-                            s_img.at[slot], r_img.at[slot], where)
+        ca[(tx, ty)] = send(img.at[rows(sx * HALF, HALF), :], img.at[rows((ty * 4 + tx) * HALF, HALF), :],
+                            0, sem_of(0, tx, ty), where)
 
     def ship_b(tx, ty, sy, where):
-        src = img.at[rows(256 + sy * HALF, HALF), :]
-        slot = tx * 4 + ty
-        cb[(tx, ty)] = send(src, img.at[rows(256 + slot * HALF, HALF), :],
-                            s_img.at[16 + slot], r_img.at[16 + slot], where)
+        cb[(tx, ty)] = send(img.at[rows(256 + sy * HALF, HALF), :],
+                            img.at[rows(256 + (tx * 4 + ty) * HALF, HALF), :],
+                            0, sem_of(1, ty, tx), where)
+
+    def pair(first, j):
+        start = first * 256 + j * 64
+        if j > 0:
+            wait_all(img.at[rows(start, 64), :], r_second.at[first * 3 + j - 1])
+        send(img.at[rows(start, 64), :], img.at[rows(512 + start, 64), :], 2, r_pair, at(dk=1))
 
     order = (1, 3, 2)
     for i in order:
@@ -131,19 +134,12 @@
         cz[(sign, step, half, c)] = send(
             txt.at[rows(TEXT_ROW[src_slot] + half * HALF, HALF), pl.ds(*CHUNKS[c])],
             txt.at[rows(TEXT_ROW[dst_slot] + half * HALF, HALF), pl.ds(*CHUNKS[c])],
-            s_z.at[n], r_z.at[n], at(dz=sign))
-
-    ck = {}
-
-    def ship_k(slot):
-        ck[slot] = send(txt.at[rows(TEXT_ROW[slot], ROWS), :], txt.at[rows(TEXT_ROW[slot] + 64, ROWS), :],
-                        s_k.at[slot], r_k.at[slot], at(dk=1))
+            1, r_z.at[n], at(dz=sign))
 
     for half in range(2):
         for c in range(2):
             ship_zc(1, 1, half, c)
             ship_zc(-1, 1, half, c)
-    ship_k(0)
 
     def forward_image(i):
         ca[(i, 0)].wait_recv()
@@ -174,24 +170,23 @@
                 cz[(-1, step, half, c)].wait_recv()
                 if step < 3 or half == 1:
                     ship_zc(-1, step + 1, half, c)
-        ship_k(8 - step)
-        ship_k(step)
         if step == 1:
             forward_image(2)
+            pair(0, 0)
+            pair(1, 0)
             pl.loop(0, 4)(select)
         if step == 2:
             pl.loop(4, 8)(select)
+            for j in (1, 3):
+                pair(0, j)
+                pair(1, j)
+        if step == 3:
+            pair(0, 2)
+            pair(1, 2)
     for c in range(2):
         cz[(1, 4, 0, c)].wait_recv()
         cz[(-1, 4, 1, c)].wait_recv()
-    ship_k(4)
-
-    for i in (0, 1, 2, 3):
-        for j in (1, 2, 3):
-            ca[(i, j)].wait_recv()
-            cb[(j, i)].wait_recv()
-    for slot in range(8):
-        ck[slot].wait_recv()
+    wait_all(img.at[rows(512, 512), :], r_pair)
 
     factor = jnp.exp(jnp.full((1, 1), scalar_ref[0], F32))
     offset = scalar_ref[1]
@@ -202,25 +197,13 @@
             txt[part, :], img[...], (((1,), (1,)), ((), ())), preferred_element_type=F32) + offset
         prob = jax.nn.sigmoid(logits)
         if i == 0:
-            row = lax.broadcasted_iota(jnp.int32, (128, ALL), 0)
-            col = lax.broadcasted_iota(jnp.int32, (128, ALL), 1)
+            row = lax.broadcasted_iota(jnp.int32, (128, IMAGES), 0)
+            col = lax.broadcasted_iota(jnp.int32, (128, IMAGES), 1)
             want = jnp.where(row < HALF, row, row + 240)
             prob = prob - jnp.where((row < ROWS) & (col == want), 1.0, 0.0).astype(F32)
         weights = (factor * prob).astype(BF16)
         wt[part, :] = weights
         tp[part, :] = jnp.dot(weights, img[...], preferred_element_type=F32).astype(BF16)
-
-    ce = {}
-
-    def give(g):
-        tile(g)
-        ce[g] = send(tp.at[rows(g * 128 + 64, 64), :], tpd.at[g], s_k.at[8 + g], r_k.at[8 + g], at(dk=1))
-
-    def join(g):
-        ce[g].wait_recv()
-        for j in range(4):
-            part = rows(g * 128 + j * HALF, HALF)
-            tp[part, :] = (tp[part, :].astype(F32) + tpd[g, rows(j * HALF, HALF), :].astype(F32)).astype(BF16)
 
     cr = {}
 
@@ -233,7 +216,7 @@
         cols = pl.ds(*CHUNKS[c])
         cr[(sign, dist, half, c)] = send(
             tp.at[rows(TEXT_ROW[slot] + half * HALF, HALF), cols], rz.at[n, :, cols],
-            s_rs.at[n * 2 + c], r_rs.at[n * 2 + c], at(dz=sign))
+            1, r_rs1 if dist == 1 else r_rs.at[n * 2 + c], at(dz=sign))
 
     def take_rs(sign, dist, half):
         slot = (dist - 1) if sign > 0 else (9 - dist)
@@ -247,60 +230,63 @@
             ship_rs(sign, dist - 1, half, c)
 
     def image_tile(i):
-        part = rows(i * 128, 128)
+        part = rows(i * 256, 256)
         ip[part, :] = lax.dot_general(
             wt[:, part], txt[...], (((0,), (0,)), ((), ())), preferred_element_type=F32).astype(BF16)
 
     ci = {}
 
     def ship_ir(name, dist, src, dst, n, where):
-        ci[(name, dist)] = send(src, dst, s_ir.at[n], r_ir.at[n], where)
-
-    give(3)
-    give(2)
-    join(3)
+        ci[(name, dist)] = send(src, dst, 4, r_ir.at[n], where)
+
+    def give_image(first):
+        image_tile(2 + first)
+        return send(ip.at[rows(512 + first * 256, 256), :], ipd.at[rows(first * 256, 256), :],
+                    3, r_ex.at[first], at(dk=1))
+
+    def join_image(first, copy):
+        copy.wait_recv()
+
+        def add(j):
+            part = rows(pl.multiple_of(first * 256 + j * ROWS, ROWS), ROWS)
+            ip[part, :] = (ip[part, :].astype(F32) + ipd[part, :].astype(F32)).astype(BF16)
+
+        pl.loop(0, 8)(add)
+
+    tile(1)
     for c in range(2):
         ship_rs(1, 4, 0, c)
         ship_rs(-1, 4, 1, c)
+        ship_rs(1, 3, 1, c)
         ship_rs(-1, 3, 0, c)
-    join(2)
-    for c in range(2):
-        ship_rs(1, 3, 1, c)
-    give(1)
-    give(0)
-    join(1)
+    tile(0)
     take_rs(1, 4, 0)
     take_rs(-1, 4, 1)
     take_rs(1, 3, 1)
     take_rs(-1, 3, 0)
-    join(0)
-
+    ex = [give_image(0), give_image(1)]
     fall[0] = fsel_ref[k * 4 + x]
-    cf = {}
     for dk in range(2):
         for dx in range(4):
             if dk == 0 and dx == 0:
                 continue
             slot = ((4 - dx) % 4) + 4 * dk
-            cf[slot] = send(fsel_ref.at[((k + dk) % 2) * 4 + (x + dx) % 4], fall.at[slot],
-                            s_f.at[slot], r_f.at[slot], at(dx=dx, dk=dk))
-
+            send(fsel_ref.at[((k + dk) % 2) * 4 + (x + dx) % 4], fall.at[slot], 6, r_f, at(dx=dx, dk=dk))
     image_tile(0)
     image_tile(1)
-    for i in order:
-        ship_ir("ay", i, ip.at[rows(i * 64, 64), :], iay.at[i - 1], i - 1, at(dy=i))
     take_rs(1, 3, 0)
     take_rs(-1, 3, 1)
     take_rs(1, 2, 1)
     take_rs(-1, 2, 0)
-    image_tile(2)
-    image_tile(3)
+    join_image(0, ex[0])
     for i in order:
-        ship_ir("bx", i, ip.at[rows(256 + i * 64, 64), :], ibx.at[i - 1], 3 + i - 1, at(dx=i))
+        ship_ir("ay", i, ip.at[rows(i * 64, 64), :], iay.at[i - 1], 0, at(dy=i))
+    join_image(1, ex[1])
+    for i in order:
+        ship_ir("bx", i, ip.at[rows(256 + i * 64, 64), :], ibx.at[i - 1], 1, at(dx=i))
 
     def fold(base, recv, name):
-        for i in order:
-            ci[(name, i)].wait_recv()
+        wait_all(recv, r_ir.at[0 if name == "ay" else 1])
         for j in range(4):
             part = rows(base + j * HALF, HALF)
             inner = rows(j * HALF, HALF)
@@ -312,10 +298,7 @@
     take_rs(1, 2, 0)
     take_rs(-1, 2, 1)
 
-    for half in range(2):
-        for sign in (1, -1):
-            for c in range(2):
-                cr[(sign, 1, half, c)].wait_recv()
+    wait_all(rz.at[pl.ds(0, 4)], r_rs1)
     halves = []
     for half in range(2):
         total = tp[rows(half * HALF, HALF), :].astype(F32)
@@ -331,8 +314,8 @@
     cp = {}
     for dx in order:
         slot = 4 - dx
-        cp[slot] = send(pall.at[0], pall.at[slot], s_p.at[slot], r_p.at[slot], at(dx=dx))
-    cp[4] = send(pall.at[0], pall.at[4], s_p.at[4], r_p.at[4], at(dk=1))
+        cp[slot] = send(pall.at[0], pall.at[slot], 5, r_p.at[slot - 1], at(dx=dx))
+    send(pall.at[0], pall.at[4], 5, r_pk, at(dk=1))
 
     gt_ref[...] = lax.dot_general(
         proj_grad, head[...], (((1,), (1,)), ((), ())), preferred_element_type=F32).astype(BF16)
@@ -344,18 +327,16 @@
     outs[1].start()
     fold(0, iay, "ay")
     for i in order:
-        ship_ir("ax", i, ip.at[rows(i * HALF, HALF), :], iax.at[i - 1], 6 + i - 1, at(dx=i))
+        ship_ir("ax", i, ip.at[rows(i * HALF, HALF), :], iax.at[i - 1], 2, at(dx=i))
     fold(256, ibx, "bx")
     for i in order:
-        ship_ir("by", i, ip.at[rows(256 + i * HALF, HALF), :], iby.at[i - 1], 9 + i - 1, at(dy=i))
+        ship_ir("by", i, ip.at[rows(256 + i * HALF, HALF), :], iby.at[i - 1], 3, at(dy=i))
 
     for slot in (1, 3, 2):
         cp[slot].wait_recv()
-        cp[4 + slot] = send(pall.at[slot], pall.at[4 + slot], s_p.at[4 + slot], r_p.at[4 + slot], at(dk=1))
-    for slot in range(4, 8):
-        cp[slot].wait_recv()
-    for slot in range(1, 8):
-        cf[slot].wait_recv()
+        send(pall.at[slot], pall.at[4 + slot], 5, r_pk, at(dk=1))
+    wait_all(pall.at[pl.ds(4, 4)], r_pk)
+    wait_all(fall.at[pl.ds(1, 7)], r_f)
 
     hp[...] = lax.dot_general(
         fall[...].reshape(256, COLS), pall[...].reshape(256, D), (((0,), (0,)), ((), ())),
@@ -364,17 +345,13 @@
         part = hp[rows(s * SLICE, SLICE), :]
         hm[s] = part[:HALF].astype(BF16)
         hl[s] = part[HALF:].astype(BF16)
-    ch = {}
-    for dz in (1, 7, 2, 6, 3, 5, 4):
+    for dz in (4, 3, 5, 2, 6, 1, 7):
         dest = (z + dz) % NZ
-        ch[dz] = (
-            send(hm.at[dest], rm.at[dz], s_h.at[dz], r_h.at[dz], at(dz=dz)),
-            send(hl.at[dest], rl.at[dz], s_h.at[8 + dz], r_h.at[8 + dz], at(dz=dz)),
-        )
-
-    for name in ("ax", "by"):
-        for i in order:
-            ci[(name, i)].wait_recv()
+        send(hm.at[dest], rm.at[dz], 7, r_hm, at(dz=dz))
+        send(hl.at[dest], rl.at[dz], 8, r_hl, at(dz=dz))
+
+    wait_all(iax, r_ir.at[2])
+    wait_all(iby, r_ir.at[3])
     total_a = ip[rows(0, HALF), :].astype(F32)
     total_b = ip[rows(256, HALF), :].astype(F32)
     for i in range(3):
@@ -391,9 +368,9 @@
     outs[0].start()
     main = hm[z].astype(F32)
     left = hl[z].astype(F32)
+    wait_all(rm.at[pl.ds(1, 7)], r_hm)
+    wait_all(rl.at[pl.ds(1, 7)], r_hl)
     for dz in (1, 7, 2, 6, 3, 5, 4):
-        for copy in ch[dz]:
-            copy.wait_recv()
         main = main + rm[dz].astype(F32)
         left = left + rl[dz].astype(F32)
     sm[...] = main.astype(BF16)
@@ -441,8 +418,18 @@
     gh_ref[pl.ds(HALF, 2), :] = left
     outs[2].start()
 
-    for copy in sent:
-        copy.wait_send()
+    for n, ref in enumerate((
+        img.at[rows(0, 480), :],
+        img.at[rows(0, 448), :],
+        img.at[rows(0, 512), :],
+        img.at[rows(0, 512), :],
+        img.at[rows(0, 480), :],
+        pall.at[pl.ds(0, 7)],
+        fall.at[pl.ds(0, 7)],
+        rm.at[pl.ds(0, 7)],
+        rl.at[pl.ds(0, 7)],
+    )):
+        wait_all(ref, s_all.at[n])
     for h in range(2):
         for tk in range(2):
             ty = k + 2 * h
@@ -495,17 +482,17 @@
             V((ROWS, D), BF16),
             V((8, ROWS, COLS), BF16),
             V((D, D), BF16),
-            V((ALL, D), BF16),
-            V((ALL, D), BF16),
-            V((ALL, ALL), BF16),
-            V((ALL, D), BF16),
-            V((ALL, D), BF16),
-            V((4, 64, D), BF16),
+            V((IMAGES, D), BF16),
+            V((TEXTS, D), BF16),
+            V((TEXTS, IMAGES), BF16),
+            V((TEXTS, D), BF16),
+            V((IMAGES, D), BF16),
             V((16, HALF, D), BF16),
             V((3, 64, D), BF16),
             V((3, HALF, D), BF16),
             V((3, 64, D), BF16),
             V((3, HALF, D), BF16),
+            V((512, D), BF16),
             V((ROWS, D), F32),
             V((8, ROWS, D), BF16),
             V((8, ROWS, COLS), BF16),
@@ -519,15 +506,8 @@
             V((4, HALF, D), BF16),
             V((4, 2, D), BF16),
             dma((3,)), dma((3,)),
-            dma((32,)), dma((32,)),
-            dma((32,)), dma((32,)),
-            dma((12,)), dma((12,)),
-            dma((8,)), dma((8,)),
-            dma((32,)), dma((32,)),
-            dma((12,)), dma((12,)),
-            dma((8,)), dma((8,)),
-            dma((16,)), dma((16,)),
-            dma((8,)), dma((8,)),
+            dma((6,)), dma((6,)), dma, dma((32,)), dma, dma((32,)), dma, dma((2,)), dma((4,)),
+            dma((3,)), dma, dma, dma, dma((8,)), dma((8,)), dma((9,)),
         ],
         compiler_params=pltpu.CompilerParams(
             collective_id=0, has_side_effects=True, vmem_limit_bytes=66500000),

time: 72 us -> 67.1 us (0.932)
  Pallas kernels: 69.3 us -> 64.4 us
    pallas_call x1, Pallas kernels: 67.6 us -> 62.7 us  [local(): pl.pallas_call(kernel, out_shape=shapes, in_specs=[pl.BlockSpec(memory_sp...]
where the time goes in v3:
time: 67.1 us; the launch traced here: 66.9 us
  Pallas kernels  64.4 us (96%)
  between operations  1.93 us (3%)
    pallas_call x1, Pallas kernels, local(): pl.pallas_call(kernel, out_shape=shapes, in_specs=[pl.BlockSpec(memory_sp...  62.7 us
    pallas_call x1, Pallas kernels, local(): pl.pallas_call(deliver, out_shape=shapes, in_specs=[hbm] * 3, out_specs=(...  1.66 us

profile of v3, /device:TPU:1, one launch (start us, length us, event | category | flops | bytes accessed | tf_op | source)
XLA Modules:
  0.0 66.9 jit_solution(494923110827179042)
XLA Ops:
  1.9 0.6 pad_maximum_fusion.scalar_ref
  2.5 62.7 %contrastive.1 = (bf16[32,1152]{1,0:T(8,128)(2,1)}, bf16[32,1152]{1,0:T(8,128)(2,1)}, f32[18,1152]{1,0:T(8,128)}) custom-call(f32[2]{0:T(128)} %pad_maximum_fusion.scalar_ref, bf16[32,1152]{1,0:T(8,128)(2,1)} %image_hbm.1, bf16[32,1152]{1,0:T(8,128)(2,1)} %text_hbm.1, bf16[1152,1152]{1,0:T(8,128)(2,1)} %head_hbm.1), custom_call_target="tpu_custom_call" | custom-call | tf_op jit(solution)/shard_map/contrastive/pallas_call | solution.py:472
  65.3 1.7 %deliver.1 = (bf16[32,1152]{1,0:T(8,128)(2,1)}, bf16[32,1152]{1,0:T(8,128)(2,1)}, f32[18,1152]{1,0:T(8,128)}) custom-call(bf16[32,1152]{1,0:T(8,128)(2,1)} %get-tuple-element.6.gi_in, bf16[32,1152]{1,0:T(8,128)(2,1)} %get-tuple-element.7.gt_in, f32[18,1152]{1,0:T(8,128)} %get-tuple-element.8.gh_in), custom_call_target="tpu_custom_call" | custom-call | tf_op jit(solution)/shard_map/deliver/pallas_call | solution.py:516

commit v4 on v3

--- a/solution.py
+++ b/solution.py
@@ -38,9 +38,9 @@
 
 
 def kernel(
-    scalar_ref, image_hbm, text_hbm, head_hbm,
+    scale_ref, bias_ref, image_hbm, text_hbm, head_hbm,
     gi_hbm, gt_hbm, gh_hbm,
-    gi_ref, gt_ref, gh_ref, image_ref, text_ref, fsel_ref, head, img, txt, wt, tp, ip, rz, iay, iax, ibx, iby,
+    gi_ref, gt_ref, gh_ref, image_ref, text_ref, fsel_ref, head, img, txt, wt, tp, ip, rz, iay, iax, iby, ibx,
     ipd, tdir, pall, fall, hp, hm, hl, rm, rl, sm, sl, qm, ql,
     in_sem, out_sem, r_first, r_second, r_pair, r_z, r_f, r_rs, r_rs1, r_ex, r_ir,
     r_p, r_pk, r_hm, r_hl, s_q, r_q, s_all,
@@ -75,7 +75,8 @@
     partners = (
         [dict(dx=i) for i in (1, 2, 3)]
         + [dict(dy=i) for i in (1, 2, 3)]
-        + [dict(dz=1), dict(dz=7), dict(dk=1)]
+        + [dict(dz=i) for i in (1, 2, 6, 7)]
+        + [dict(dk=1)]
     )
     for p in partners:
         pl.semaphore_signal(barrier, inc=1, device_id=at(**p), device_id_type=MESH)
@@ -128,13 +129,14 @@
     cz = {}
 
     def ship_zc(sign, step, half, c):
-        src_slot = ((8 - (step - 1)) % 8) if sign > 0 else step - 1
+        before = min(step - 1, 2)
+        src_slot = ((8 - before) % 8) if sign > 0 else before
         dst_slot = (8 - step) if sign > 0 else step
         n = (((0 if sign > 0 else 4) + step - 1) * 2 + half) * 2 + c
         cz[(sign, step, half, c)] = send(
             txt.at[rows(TEXT_ROW[src_slot] + half * HALF, HALF), pl.ds(*CHUNKS[c])],
             txt.at[rows(TEXT_ROW[dst_slot] + half * HALF, HALF), pl.ds(*CHUNKS[c])],
-            1, r_z.at[n], at(dz=sign))
+            1, r_z.at[n], at(dz=sign * (step - before)))
 
     for half in range(2):
         for c in range(2):
@@ -164,12 +166,12 @@
     for step in (1, 2, 3):
         for half in range(2):
             for c in range(2):
-                cz[(1, step, half, c)].wait_recv()
-                if step < 3 or half == 0:
-                    ship_zc(1, step + 1, half, c)
-                cz[(-1, step, half, c)].wait_recv()
-                if step < 3 or half == 1:
-                    ship_zc(-1, step + 1, half, c)
+                for sign in (1, -1):
+                    cz[(sign, step, half, c)].wait_recv()
+                    if step == 2 and half == (0 if sign > 0 else 1):
+                        ship_zc(sign, 4, half, c)
+                    if step < 3:
+                        ship_zc(sign, step + 1, half, c)
         if step == 1:
             forward_image(2)
             pair(0, 0)
@@ -186,24 +188,25 @@
     for c in range(2):
         cz[(1, 4, 0, c)].wait_recv()
         cz[(-1, 4, 1, c)].wait_recv()
-    wait_all(img.at[rows(512, 512), :], r_pair)
-
-    factor = jnp.exp(jnp.full((1, 1), scalar_ref[0], F32))
-    offset = scalar_ref[1]
+    factor = jnp.exp(jnp.full((1, 1), scale_ref[0], F32))
+    offset = bias_ref[0]
+
+    def weigh(i, core):
+        part = rows(i * 128, 128)
+        logits = factor * lax.dot_general(
+            txt[part, :], img[rows(core * 512, 512), :], (((1,), (1,)), ((), ())),
+            preferred_element_type=F32) + offset
+        prob = jax.nn.sigmoid(logits)
+        if i == 0 and core == 0:
+            row = lax.broadcasted_iota(jnp.int32, (128, 512), 0)
+            col = lax.broadcasted_iota(jnp.int32, (128, 512), 1)
+            want = jnp.where(row < HALF, row, row + 240)
+            prob = prob - jnp.where((row < ROWS) & (col == want), 1.0, 0.0).astype(F32)
+        wt[part, pl.ds(core * 512, 512)] = (factor * prob).astype(BF16)
 
     def tile(i):
         part = rows(i * 128, 128)
-        logits = factor * lax.dot_general(
-            txt[part, :], img[...], (((1,), (1,)), ((), ())), preferred_element_type=F32) + offset
-        prob = jax.nn.sigmoid(logits)
-        if i == 0:
-            row = lax.broadcasted_iota(jnp.int32, (128, IMAGES), 0)
-            col = lax.broadcasted_iota(jnp.int32, (128, IMAGES), 1)
-            want = jnp.where(row < HALF, row, row + 240)
-            prob = prob - jnp.where((row < ROWS) & (col == want), 1.0, 0.0).astype(F32)
-        weights = (factor * prob).astype(BF16)
-        wt[part, :] = weights
-        tp[part, :] = jnp.dot(weights, img[...], preferred_element_type=F32).astype(BF16)
+        tp[part, :] = jnp.dot(wt[part, :], img[...], preferred_element_type=F32).astype(BF16)
 
     cr = {}
 
@@ -216,18 +219,19 @@
         cols = pl.ds(*CHUNKS[c])
         cr[(sign, dist, half, c)] = send(
             tp.at[rows(TEXT_ROW[slot] + half * HALF, HALF), cols], rz.at[n, :, cols],
-            1, r_rs1 if dist == 1 else r_rs.at[n * 2 + c], at(dz=sign))
-
-    def take_rs(sign, dist, half):
-        slot = (dist - 1) if sign > 0 else (9 - dist)
+            1, r_rs1 if dist == 1 else r_rs.at[n * 2 + c], at(dz=sign * (2 if dist == 4 else 1)))
+
+    def take_rs(sign, dists, half, c):
+        to = 2 if 4 in dists or 3 in dists else 1
+        slot = to if sign > 0 else 8 - to
         part = rows(TEXT_ROW[slot] + half * HALF, HALF)
-        for c in range(2):
-            cols = pl.ds(*CHUNKS[c])
+        cols = pl.ds(*CHUNKS[c])
+        total = tp[part, cols].astype(F32)
+        for dist in dists:
             cr[(sign, dist, half, c)].wait_recv()
-            tp[part, cols] = (
-                tp[part, cols].astype(F32) + rz[rz_slot(sign, dist, half), :, cols].astype(F32)
-            ).astype(BF16)
-            ship_rs(sign, dist - 1, half, c)
+            total = total + rz[rz_slot(sign, dist, half), :, cols].astype(F32)
+        tp[part, cols] = total.astype(BF16)
+        ship_rs(sign, to, half, c)
 
     def image_tile(i):
         part = rows(i * 256, 256)
@@ -253,18 +257,39 @@
 
         pl.loop(0, 8)(add)
 
+    weigh(1, 0)
+    wait_all(img.at[rows(512, 512), :], r_pair)
+    weigh(1, 1)
     tile(1)
     for c in range(2):
         ship_rs(1, 4, 0, c)
         ship_rs(-1, 4, 1, c)
-        ship_rs(1, 3, 1, c)
-        ship_rs(-1, 3, 0, c)
+        for half in range(2):
+            ship_rs(1, 3, half, c)
+            ship_rs(-1, 3, half, c)
+    weigh(0, 0)
+    weigh(0, 1)
     tile(0)
-    take_rs(1, 4, 0)
-    take_rs(-1, 4, 1)
-    take_rs(1, 3, 1)
-    take_rs(-1, 3, 0)
     ex = [give_image(0), give_image(1)]
+    image_tile(0)
+    image_tile(1)
+    join_image(0, ex[0])
+    for i in order:
+        ship_ir("ay", i, ip.at[rows(i * 64, 64), :], iay.at[i - 1], 0, at(dy=i))
+    join_image(1, ex[1])
+    for i in order:
+        for j in range(4):
+            ship_ir("by", i, ip.at[rows(256 + j * 64 + i * HALF, HALF), :],
+                    iby.at[i - 1, rows(j * HALF, HALF), :], 1, at(dy=i))
+    for c in range(2):
+        take_rs(1, (4, 3), 0, c)
+        take_rs(-1, (4, 3), 1, c)
+        take_rs(1, (3,), 1, c)
+        take_rs(-1, (3,), 0, c)
+    for c in range(2):
+        for half in range(2):
+            take_rs(1, (2,), half, c)
+            take_rs(-1, (2,), half, c)
     fall[0] = fsel_ref[k * 4 + x]
     for dk in range(2):
         for dx in range(4):
@@ -272,31 +297,15 @@
                 continue
             slot = ((4 - dx) % 4) + 4 * dk
             send(fsel_ref.at[((k + dk) % 2) * 4 + (x + dx) % 4], fall.at[slot], 6, r_f, at(dx=dx, dk=dk))
-    image_tile(0)
-    image_tile(1)
-    take_rs(1, 3, 0)
-    take_rs(-1, 3, 1)
-    take_rs(1, 2, 1)
-    take_rs(-1, 2, 0)
-    join_image(0, ex[0])
-    for i in order:
-        ship_ir("ay", i, ip.at[rows(i * 64, 64), :], iay.at[i - 1], 0, at(dy=i))
-    join_image(1, ex[1])
-    for i in order:
-        ship_ir("bx", i, ip.at[rows(256 + i * 64, 64), :], ibx.at[i - 1], 1, at(dx=i))
-
-    def fold(base, recv, name):
-        wait_all(recv, r_ir.at[0 if name == "ay" else 1])
+
+    def fold(base, step, recv, sem):
+        wait_all(recv, sem)
         for j in range(4):
-            part = rows(base + j * HALF, HALF)
-            inner = rows(j * HALF, HALF)
+            part = rows(base + j * step, HALF)
             total = ip[part, :].astype(F32)
             for i in range(3):
-                total = total + recv[i, inner, :].astype(F32)
+                total = total + recv[i, rows(j * HALF, HALF), :].astype(F32)
             ip[part, :] = total.astype(BF16)
-
-    take_rs(1, 2, 0)
-    take_rs(-1, 2, 1)
 
     wait_all(rz.at[pl.ds(0, 4)], r_rs1)
     halves = []
@@ -325,13 +334,6 @@
         for n, (src, dst) in enumerate(((gi_ref, gi_hbm), (gt_ref, gt_hbm), (gh_ref, gh_hbm)))
     ]
     outs[1].start()
-    fold(0, iay, "ay")
-    for i in order:
-        ship_ir("ax", i, ip.at[rows(i * HALF, HALF), :], iax.at[i - 1], 2, at(dx=i))
-    fold(256, ibx, "bx")
-    for i in order:
-        ship_ir("by", i, ip.at[rows(256 + i * HALF, HALF), :], iby.at[i - 1], 3, at(dy=i))
-
     for slot in (1, 3, 2):
         cp[slot].wait_recv()
         send(pall.at[slot], pall.at[4 + slot], 5, r_pk, at(dk=1))
@@ -350,13 +352,18 @@
         send(hm.at[dest], rm.at[dz], 7, r_hm, at(dz=dz))
         send(hl.at[dest], rl.at[dz], 8, r_hl, at(dz=dz))
 
+    fold(0, HALF, iay, r_ir.at[0])
+    fold(256, 64, iby, r_ir.at[1])
+    for i in order:
+        ship_ir("ax", i, ip.at[rows(i * HALF, HALF), :], iax.at[i - 1], 2, at(dx=i))
+        ship_ir("bx", i, ip.at[rows(256 + i * 64, HALF), :], ibx.at[i - 1], 3, at(dx=i))
     wait_all(iax, r_ir.at[2])
-    wait_all(iby, r_ir.at[3])
+    wait_all(ibx, r_ir.at[3])
     total_a = ip[rows(0, HALF), :].astype(F32)
     total_b = ip[rows(256, HALF), :].astype(F32)
     for i in range(3):
         total_a = total_a + iax[i].astype(F32)
-        total_b = total_b + iby[i].astype(F32)
+        total_b = total_b + ibx[i].astype(F32)
     image_sum = jnp.concatenate([total_a, total_b], axis=0)
     wide = image_ref[...].astype(F32)
     image_len = jnp.sqrt(jnp.sum(wide * wide, axis=-1, keepdims=True) + EPSILON)
@@ -472,7 +479,7 @@
     results = pl.pallas_call(
         kernel,
         out_shape=shapes,
-        in_specs=[pl.BlockSpec(memory_space=pltpu.SMEM)] + [hbm] * 3,
+        in_specs=[pl.BlockSpec(memory_space=pltpu.SMEM)] * 2 + [hbm] * 3,
         out_specs=(hbm, hbm, hbm),
         scratch_shapes=[
             V((ROWS, D), BF16),
@@ -512,7 +519,7 @@
         compiler_params=pltpu.CompilerParams(
             collective_id=0, has_side_effects=True, vmem_limit_bytes=66500000),
         name="contrastive",
-    )(jnp.concatenate([log_scale, bias]), image_embed, text_feature, text_head)
+    )(log_scale, bias, image_embed, text_feature, text_head)
     return pl.pallas_call(
         deliver,
         out_shape=shapes,

time: 67.1 us -> 62.3 us (0.928)
  Pallas kernels: 64.4 us -> 60.2 us
    pallas_call x1, Pallas kernels: 62.7 us -> 58.5 us  [local(): pl.pallas_call(kernel, out_shape=shapes, in_specs=[pl.BlockSpec(memory_sp...]
where the time goes in v4:
time: 62.3 us; the launch traced here: 62.1 us
  Pallas kernels  60.2 us (97%)
  between operations  1.93 us (3%)
    pallas_call x1, Pallas kernels, local(): pl.pallas_call(kernel, out_shape=shapes, in_specs=[pl.BlockSpec(memory_sp...  58.5 us
    pallas_call x1, Pallas kernels, local(): pl.pallas_call(deliver, out_shape=shapes, in_specs=[hbm] * 3, out_specs=(...  1.66 us

profile of v4, /device:TPU:1, one launch (start us, length us, event | category | flops | bytes accessed | tf_op | source)
XLA Modules:
  0.0 62.1 jit_solution(8877146516510981036)
XLA Ops:
  1.9 58.5 %contrastive.1 = (bf16[32,1152]{1,0:T(8,128)(2,1)}, bf16[32,1152]{1,0:T(8,128)(2,1)}, f32[18,1152]{1,0:T(8,128)}) custom-call(f32[1]{0:T(128)S(6)} %copy.8.scale_ref, f32[1]{0:T(128)S(6)} %copy.9.bias_ref, bf16[32,1152]{1,0:T(8,128)(2,1)} %image_hbm.1, bf16[32,1152]{1,0:T(8,128)(2,1)} %text_hbm.1, bf16[1152,1152]{1,0:T(8,128)(2,1)} %head_hbm.1), custom_call_target="tpu_custom_call" | custom-call | tf_op jit(solution)/shard_map/contrastive/pallas_call | solution.py:479
  60.5 1.7 %deliver.1 = (bf16[32,1152]{1,0:T(8,128)(2,1)}, bf16[32,1152]{1,0:T(8,128)(2,1)}, f32[18,1152]{1,0:T(8,128)}) custom-call(bf16[32,1152]{1,0:T(8,128)(2,1)} %get-tuple-element.6.gi_in, bf16[32,1152]{1,0:T(8,128)(2,1)} %get-tuple-element.7.gt_in, f32[18,1152]{1,0:T(8,128)} %get-tuple-element.8.gh_in), custom_call_target="tpu_custom_call" | custom-call | tf_op jit(solution)/shard_map/deliver/pallas_call | solution.py:523

commit v5 on v4

--- a/solution.py
+++ b/solution.py
@@ -39,10 +39,9 @@
 
 def kernel(
     scale_ref, bias_ref, image_hbm, text_hbm, head_hbm,
-    gi_hbm, gt_hbm, gh_hbm,
     gi_ref, gt_ref, gh_ref, image_ref, text_ref, fsel_ref, head, img, txt, wt, tp, ip, rz, iay, iax, iby, ibx,
     ipd, tdir, pall, fall, hp, hm, hl, rm, rl, sm, sl, qm, ql,
-    in_sem, out_sem, r_first, r_second, r_pair, r_z, r_f, r_rs, r_rs1, r_ex, r_ir,
+    in_sem, r_first, r_second, r_pair, r_z, r_f, r_rs, r_rs1, r_ex, r_ir,
     r_p, r_pk, r_hm, r_hl, s_q, r_q, s_all,
 ):
     x, y, z, k = place()
@@ -132,7 +131,7 @@
         before = min(step - 1, 2)
         src_slot = ((8 - before) % 8) if sign > 0 else before
         dst_slot = (8 - step) if sign > 0 else step
-        n = (((0 if sign > 0 else 4) + step - 1) * 2 + half) * 2 + c
+        n = 16 if step > 2 else (((0 if sign > 0 else 2) + step - 1) * 2 + half) * 2 + c
         cz[(sign, step, half, c)] = send(
             txt.at[rows(TEXT_ROW[src_slot] + half * HALF, HALF), pl.ds(*CHUNKS[c])],
             txt.at[rows(TEXT_ROW[dst_slot] + half * HALF, HALF), pl.ds(*CHUNKS[c])],
@@ -163,31 +162,25 @@
 
     forward_image(3)
     forward_image(1)
-    for step in (1, 2, 3):
+    for step in (1, 2):
         for half in range(2):
             for c in range(2):
                 for sign in (1, -1):
                     cz[(sign, step, half, c)].wait_recv()
                     if step == 2 and half == (0 if sign > 0 else 1):
                         ship_zc(sign, 4, half, c)
-                    if step < 3:
-                        ship_zc(sign, step + 1, half, c)
+                    ship_zc(sign, step + 1, half, c)
         if step == 1:
             forward_image(2)
             pair(0, 0)
             pair(1, 0)
             pl.loop(0, 4)(select)
-        if step == 2:
-            pl.loop(4, 8)(select)
-            for j in (1, 3):
-                pair(0, j)
-                pair(1, j)
-        if step == 3:
-            pair(0, 2)
-            pair(1, 2)
-    for c in range(2):
-        cz[(1, 4, 0, c)].wait_recv()
-        cz[(-1, 4, 1, c)].wait_recv()
+    pl.loop(4, 8)(select)
+    for j in (1, 3, 2):
+        pair(0, j)
+        pair(1, j)
+    wait_all(txt.at[rows(0, 96), :], r_z.at[16])
+
     factor = jnp.exp(jnp.full((1, 1), scale_ref[0], F32))
     offset = bias_ref[0]
 
@@ -216,10 +209,13 @@
     def ship_rs(sign, dist, half, c):
         slot = dist if sign > 0 else (8 - dist)
         n = rz_slot(sign, dist, half)
+        m = ((0 if sign > 0 else 2) + half) * 2 + c + 4 + 8 * (3 - dist)
+        if dist == 4:
+            m = (0 if sign > 0 else 2) + c
         cols = pl.ds(*CHUNKS[c])
         cr[(sign, dist, half, c)] = send(
             tp.at[rows(TEXT_ROW[slot] + half * HALF, HALF), cols], rz.at[n, :, cols],
-            1, r_rs1 if dist == 1 else r_rs.at[n * 2 + c], at(dz=sign * (2 if dist == 4 else 1)))
+            1, r_rs1 if dist == 1 else r_rs.at[m], at(dz=sign * (2 if dist == 4 else 1)))
 
     def take_rs(sign, dists, half, c):
         to = 2 if 4 in dists or 3 in dists else 1
@@ -258,6 +254,7 @@
         pl.loop(0, 8)(add)
 
     weigh(1, 0)
+    weigh(0, 0)
     wait_all(img.at[rows(512, 512), :], r_pair)
     weigh(1, 1)
     tile(1)
@@ -267,7 +264,6 @@
         for half in range(2):
             ship_rs(1, 3, half, c)
             ship_rs(-1, 3, half, c)
-    weigh(0, 0)
     weigh(0, 1)
     tile(0)
     ex = [give_image(0), give_image(1)]
@@ -329,11 +325,6 @@
     gt_ref[...] = lax.dot_general(
         proj_grad, head[...], (((1,), (1,)), ((), ())), preferred_element_type=F32).astype(BF16)
 
-    outs = [
-        pltpu.make_async_copy(src, dst, out_sem.at[n])
-        for n, (src, dst) in enumerate(((gi_ref, gi_hbm), (gt_ref, gt_hbm), (gh_ref, gh_hbm)))
-    ]
-    outs[1].start()
     for slot in (1, 3, 2):
         cp[slot].wait_recv()
         send(pall.at[slot], pall.at[4 + slot], 5, r_pk, at(dk=1))
@@ -347,10 +338,14 @@
         part = hp[rows(s * SLICE, SLICE), :]
         hm[s] = part[:HALF].astype(BF16)
         hl[s] = part[HALF:].astype(BF16)
-    for dz in (4, 3, 5, 2, 6, 1, 7):
-        dest = (z + dz) % NZ
-        send(hm.at[dest], rm.at[dz], 7, r_hm, at(dz=dz))
-        send(hl.at[dest], rl.at[dz], 8, r_hl, at(dz=dz))
+    far = (4, 3, 5, 2, 6, 1, 7)
+    for c in range(2):
+        cols = pl.ds(*CHUNKS[c])
+        for dz in far:
+            dest = (z + dz) % NZ
+            send(hm.at[dest, :, cols], rm.at[dz, :, cols], 7, r_hm.at[c], at(dz=dz))
+            if c == 0:
+                send(hl.at[dest], rl.at[dz], 8, r_hl, at(dz=dz))
 
     fold(0, HALF, iay, r_ir.at[0])
     fold(256, 64, iby, r_ir.at[1])
@@ -372,58 +367,69 @@
         (image_sum - image_dir * jnp.sum(image_dir * image_sum, axis=-1, keepdims=True)) / image_len
     ).astype(BF16)
 
-    outs[0].start()
-    main = hm[z].astype(F32)
-    left = hl[z].astype(F32)
-    wait_all(rm.at[pl.ds(1, 7)], r_hm)
-    wait_all(rl.at[pl.ds(1, 7)], r_hl)
-    for dz in (1, 7, 2, 6, 3, 5, 4):
-        main = main + rm[dz].astype(F32)
-        left = left + rl[dz].astype(F32)
-    sm[...] = main.astype(BF16)
-    sl[...] = left.astype(BF16)
-
     y_lo = y % 2
 
-    def final(target_y, target_k, slot):
-        return (
-            pltpu.make_async_remote_copy(
-                src_ref=sm, dst_ref=qm.at[slot], send_sem=s_q.at[target_y // 2 * 2 + target_k],
-                recv_sem=r_q.at[slot], device_id=device(x, target_y, z, target_k), device_id_type=MESH),
-            pltpu.make_async_remote_copy(
-                src_ref=sl, dst_ref=ql.at[slot], send_sem=s_q.at[4 + target_y // 2 * 2 + target_k],
-                recv_sem=r_q.at[4 + slot], device_id=device(x, target_y, z, target_k), device_id_type=MESH),
-        )
-
-    for h in range(2):
-        for tk in range(2):
-            ty = k + 2 * h
-            own = (ty == y) & (tk == k)
-
-            @pl.when(jnp.logical_not(own))
+    def piece(p, slot):
+        if p == 2:
+            return sl, ql.at[slot]
+        return sm.at[:, pl.ds(*CHUNKS[p])], qm.at[slot, :, pl.ds(*CHUNKS[p])]
+
+    def final(p, target_y, target_k, slot):
+        src, dst = piece(p, slot)
+        return pltpu.make_async_remote_copy(
+            src_ref=src, dst_ref=dst, send_sem=s_q.at[p * 4 + target_y // 2 * 2 + target_k],
+            recv_sem=r_q.at[p * 4 + slot], device_id=device(x, target_y, z, target_k), device_id_type=MESH)
+
+    def scatter(pieces):
+        for h in range(2):
+            for tk in range(2):
+                ty = k + 2 * h
+                own = (ty == y) & (tk == k)
+
+                @pl.when(jnp.logical_not(own))
+                def _():
+                    for p in pieces:
+                        final(p, ty, tk, y).start()
+
+                @pl.when(own)
+                def _():
+                    for p in pieces:
+                        src, dst = piece(p, y)
+                        dst[...] = src[...]
+
+    def collect(pieces):
+        for sy in range(4):
+            @pl.when(jnp.logical_not((sy == y) & (k == y_lo)))
             def _():
-                for copy in final(ty, tk, y):
-                    copy.start()
-
-            @pl.when(own)
-            def _():
-                qm[y] = sm[...]
-                ql[y] = sl[...]
-
-    for sy in range(4):
-        @pl.when(jnp.logical_not((sy == y) & (k == y_lo)))
-        def _():
-            for copy in final(y, k, sy):
-                copy.wait_recv()
-
-    main = qm[0].astype(F32)
-    left = ql[0].astype(F32)
-    for sy in range(1, 4):
-        main = main + qm[sy].astype(F32)
-        left = left + ql[sy].astype(F32)
-    gh_ref[pl.ds(0, HALF), :] = main
-    gh_ref[pl.ds(HALF, 2), :] = left
-    outs[2].start()
+                for p in pieces:
+                    final(p, y, k, sy).wait_recv()
+
+    def sum_z(own, recv):
+        total = own.astype(F32)
+        for dz in far:
+            total = total + recv(dz).astype(F32)
+        return total.astype(BF16)
+
+    def sum_y(part):
+        total = part(0).astype(F32)
+        for sy in range(1, 4):
+            total = total + part(sy).astype(F32)
+        return total
+
+    for c in range(2):
+        cols = pl.ds(*CHUNKS[c])
+        wait_all(rm.at[pl.ds(1, 7), :, cols], r_hm.at[c])
+        sm[:, cols] = sum_z(hm[z, :, cols], lambda dz: rm[dz, :, cols])
+        if c == 0:
+            wait_all(rl.at[pl.ds(1, 7)], r_hl)
+            sl[...] = sum_z(hl[z], lambda dz: rl[dz])
+        scatter((0, 2) if c == 0 else (1,))
+    for c in range(2):
+        cols = pl.ds(*CHUNKS[c])
+        collect((0, 2) if c == 0 else (1,))
+        gh_ref[pl.ds(0, HALF), cols] = sum_y(lambda sy: qm[sy, :, cols])
+        if c == 0:
+            gh_ref[pl.ds(HALF, 2), :] = sum_y(lambda sy: ql[sy])
 
     for n, ref in enumerate((
         img.at[rows(0, 480), :],
@@ -443,32 +449,24 @@
 
             @pl.when(jnp.logical_not((ty == y) & (tk == k)))
             def _():
-                for copy in final(ty, tk, y):
-                    copy.wait_send()
-    for copy in outs:
-        copy.wait()
-
-
-def deliver(gi_in, gt_in, gh_in, gi_out, gt_out, gh_out, gi_ref, gt_ref, gh_ref, in_sem, out_sem):
-    first = [
-        pltpu.make_async_copy(src, dst, in_sem.at[n])
-        for n, (src, dst) in enumerate(((gi_in, gi_ref), (gt_in, gt_ref), (gh_in, gh_ref)))
-    ]
-    second = [
-        pltpu.make_async_copy(src, dst, out_sem.at[n])
+                for p in range(3):
+                    final(p, ty, tk, y).wait_send()
+
+
+def deliver(gi_ref, gt_ref, gh_ref, gi_out, gt_out, gh_out, sem):
+    copies = [
+        pltpu.make_async_copy(src, dst, sem.at[n])
         for n, (src, dst) in enumerate(((gi_ref, gi_out), (gt_ref, gt_out), (gh_ref, gh_out)))
     ]
-    for copy in first:
+    for copy in copies:
         copy.start()
-    for n in range(3):
-        first[n].wait()
-        second[n].start()
-    for copy in second:
+    for copy in copies:
         copy.wait()
 
 
 def local(image_embed, text_feature, text_head, log_scale, bias):
     hbm = pl.BlockSpec(memory_space=pltpu.HBM)
+    vmem = pl.BlockSpec(memory_space=pltpu.VMEM)
     dma = pltpu.SemaphoreType.DMA
     V = pltpu.VMEM
     shapes = (
@@ -478,13 +476,10 @@
     )
     results = pl.pallas_call(
         kernel,
-        out_shape=shapes,
+        out_shape=tuple(pltpu.VMEM(a.shape, a.dtype) for a in shapes),
         in_specs=[pl.BlockSpec(memory_space=pltpu.SMEM)] * 2 + [hbm] * 3,
-        out_specs=(hbm, hbm, hbm),
+        out_specs=(vmem, vmem, vmem),
         scratch_shapes=[
-            V((ROWS, D), BF16),
-            V((ROWS, D), BF16),
-            V((SLICE, D), F32),
             V((ROWS, D), BF16),
             V((ROWS, D), BF16),
             V((8, ROWS, COLS), BF16),
@@ -512,9 +507,9 @@
             V((2, D), BF16),
             V((4, HALF, D), BF16),
             V((4, 2, D), BF16),
-            dma((3,)), dma((3,)),
-            dma((6,)), dma((6,)), dma, dma((32,)), dma, dma((32,)), dma, dma((2,)), dma((4,)),
-            dma((3,)), dma, dma, dma, dma((8,)), dma((8,)), dma((9,)),
+            dma((3,)),
+            dma((6,)), dma((6,)), dma, dma((17,)), dma, dma((20,)), dma, dma((2,)), dma((4,)),
+            dma((3,)), dma, dma((2,)), dma, dma((12,)), dma((12,)), dma((9,)),
         ],
         compiler_params=pltpu.CompilerParams(
             collective_id=0, has_side_effects=True, vmem_limit_bytes=66500000),
@@ -523,11 +518,10 @@
     return pl.pallas_call(
         deliver,
         out_shape=shapes,
-        in_specs=[hbm] * 3,
+        in_specs=[vmem] * 3,
         out_specs=(hbm, hbm, hbm),
-        scratch_shapes=[
-            V((ROWS, D), BF16), V((ROWS, D), BF16), V((SLICE, D), F32), dma((3,)), dma((3,))],
-        compiler_params=pltpu.CompilerParams(vmem_limit_bytes=66500000),
+        scratch_shapes=[dma((3,))],
+        compiler_params=pltpu.CompilerParams(vmem_limit_bytes=2**20),
         name="deliver",
     )(*results)
 

time: 62.3 us -> 59.1 us (0.949)
  Pallas kernels: 60.2 us -> 57.1 us
    pallas_call x2, Pallas kernels: 60.2 us -> 57.1 us  [the longest x1 56.4 us: local(): pl.pallas_call(kernel, out_shape=tuple((pltpu.VMEM(a.shape, a.dtype) for...]
where the time goes in v5:
time: 59.1 us; the launch traced here: 59 us
  Pallas kernels  57.1 us (97%)
  between operations  1.93 us (3%)
    pallas_call x1, Pallas kernels, local(): pl.pallas_call(kernel, out_shape=tuple((pltpu.VMEM(a.shape, a.dtype) for...  56.4 us

profile of v5, /device:TPU:1, one launch (start us, length us, event | category | flops | bytes accessed | tf_op | source)
XLA Modules:
  0.0 59.0 jit_solution(18246390531034762564)
XLA Ops:
  1.9 56.4 %contrastive.1 = (bf16[32,1152]{1,0:T(8,128)(2,1)S(1)}, bf16[32,1152]{1,0:T(8,128)(2,1)S(1)}, f32[18,1152]{1,0:T(8,128)S(1)}) custom-call(f32[1]{0:T(128)S(6)} %copy.8.scale_ref, f32[1]{0:T(128)S(6)} %copy.9.bias_ref, bf16[32,1152]{1,0:T(8,128)(2,1)} %image_hbm.1, bf16[32,1152]{1,0:T(8,128)(2,1)} %text_hbm.1, bf16[1152,1152]{1,0:T(8,128)(2,1)} %head_hbm.1), custom_call_target="tpu_custom_call" | custom-call | tf_op jit(solution)/shard_map/contrastive/pallas_call | solution.py:477
  58.3 0.7 %deliver.1 = (bf16[32,1152]{1,0:T(8,128)(2,1)}, bf16[32,1152]{1,0:T(8,128)(2,1)}, f32[18,1152]{1,0:T(8,128)}) custom-call(bf16[32,1152]{1,0:T(8,128)(2,1)S(1)} %get-tuple-element.6.gi_ref, bf16[32,1152]{1,0:T(8,128)(2,1)S(1)} %get-tuple-element.7.gt_ref, f32[18,1152]{1,0:T(8,128)S(1)} %get-tuple-element.8.gh_ref), custom_call_target="tpu_custom_call" | custom-call | tf_op jit(solution)/shard_map/deliver/pallas_call | solution.py:518

commit v6 on v5

--- a/solution.py
+++ b/solution.py
@@ -31,6 +31,7 @@
 TEXTS = 256
 IMAGES = 1024
 CHUNKS = ((0, 640), (640, 512))
+PIECES = ((0, 768), (768, 384))
 
 
 def rows(start, count):
@@ -179,8 +180,6 @@
     for j in (1, 3, 2):
         pair(0, j)
         pair(1, j)
-    wait_all(txt.at[rows(0, 96), :], r_z.at[16])
-
     factor = jnp.exp(jnp.full((1, 1), scale_ref[0], F32))
     offset = bias_ref[0]
 
@@ -253,8 +252,9 @@
 
         pl.loop(0, 8)(add)
 
+    weigh(0, 0)
+    wait_all(txt.at[rows(0, 96), :], r_z.at[16])
     weigh(1, 0)
-    weigh(0, 0)
     wait_all(img.at[rows(512, 512), :], r_pair)
     weigh(1, 1)
     tile(1)
@@ -269,6 +269,11 @@
     ex = [give_image(0), give_image(1)]
     image_tile(0)
     image_tile(1)
+    for c in range(2):
+        take_rs(1, (4, 3), 0, c)
+        take_rs(-1, (4, 3), 1, c)
+        take_rs(1, (3,), 1, c)
+        take_rs(-1, (3,), 0, c)
     join_image(0, ex[0])
     for i in order:
         ship_ir("ay", i, ip.at[rows(i * 64, 64), :], iay.at[i - 1], 0, at(dy=i))
@@ -277,11 +282,6 @@
         for j in range(4):
             ship_ir("by", i, ip.at[rows(256 + j * 64 + i * HALF, HALF), :],
                     iby.at[i - 1, rows(j * HALF, HALF), :], 1, at(dy=i))
-    for c in range(2):
-        take_rs(1, (4, 3), 0, c)
-        take_rs(-1, (4, 3), 1, c)
-        take_rs(1, (3,), 1, c)
-        take_rs(-1, (3,), 0, c)
     for c in range(2):
         for half in range(2):
             take_rs(1, (2,), half, c)
@@ -340,7 +340,7 @@
         hl[s] = part[HALF:].astype(BF16)
     far = (4, 3, 5, 2, 6, 1, 7)
     for c in range(2):
-        cols = pl.ds(*CHUNKS[c])
+        cols = pl.ds(*PIECES[c])
         for dz in far:
             dest = (z + dz) % NZ
             send(hm.at[dest, :, cols], rm.at[dz, :, cols], 7, r_hm.at[c], at(dz=dz))
@@ -352,27 +352,12 @@
     for i in order:
         ship_ir("ax", i, ip.at[rows(i * HALF, HALF), :], iax.at[i - 1], 2, at(dx=i))
         ship_ir("bx", i, ip.at[rows(256 + i * 64, HALF), :], ibx.at[i - 1], 3, at(dx=i))
-    wait_all(iax, r_ir.at[2])
-    wait_all(ibx, r_ir.at[3])
-    total_a = ip[rows(0, HALF), :].astype(F32)
-    total_b = ip[rows(256, HALF), :].astype(F32)
-    for i in range(3):
-        total_a = total_a + iax[i].astype(F32)
-        total_b = total_b + ibx[i].astype(F32)
-    image_sum = jnp.concatenate([total_a, total_b], axis=0)
-    wide = image_ref[...].astype(F32)
-    image_len = jnp.sqrt(jnp.sum(wide * wide, axis=-1, keepdims=True) + EPSILON)
-    image_dir = wide / image_len
-    gi_ref[...] = (
-        (image_sum - image_dir * jnp.sum(image_dir * image_sum, axis=-1, keepdims=True)) / image_len
-    ).astype(BF16)
-
     y_lo = y % 2
 
     def piece(p, slot):
         if p == 2:
             return sl, ql.at[slot]
-        return sm.at[:, pl.ds(*CHUNKS[p])], qm.at[slot, :, pl.ds(*CHUNKS[p])]
+        return sm.at[:, pl.ds(*PIECES[p])], qm.at[slot, :, pl.ds(*PIECES[p])]
 
     def final(p, target_y, target_k, slot):
         src, dst = piece(p, slot)
@@ -416,16 +401,34 @@
             total = total + part(sy).astype(F32)
         return total
 
+    def finish_image():
+        wait_all(iax, r_ir.at[2])
+        wait_all(ibx, r_ir.at[3])
+        total_a = ip[rows(0, HALF), :].astype(F32)
+        total_b = ip[rows(256, HALF), :].astype(F32)
+        for i in range(3):
+            total_a = total_a + iax[i].astype(F32)
+            total_b = total_b + ibx[i].astype(F32)
+        image_sum = jnp.concatenate([total_a, total_b], axis=0)
+        wide = image_ref[...].astype(F32)
+        image_len = jnp.sqrt(jnp.sum(wide * wide, axis=-1, keepdims=True) + EPSILON)
+        image_dir = wide / image_len
+        gi_ref[...] = (
+            (image_sum - image_dir * jnp.sum(image_dir * image_sum, axis=-1, keepdims=True)) / image_len
+        ).astype(BF16)
+
     for c in range(2):
-        cols = pl.ds(*CHUNKS[c])
+        cols = pl.ds(*PIECES[c])
         wait_all(rm.at[pl.ds(1, 7), :, cols], r_hm.at[c])
         sm[:, cols] = sum_z(hm[z, :, cols], lambda dz: rm[dz, :, cols])
         if c == 0:
             wait_all(rl.at[pl.ds(1, 7)], r_hl)
             sl[...] = sum_z(hl[z], lambda dz: rl[dz])
         scatter((0, 2) if c == 0 else (1,))
+        if c == 0:
+            finish_image()
     for c in range(2):
-        cols = pl.ds(*CHUNKS[c])
+        cols = pl.ds(*PIECES[c])
         collect((0, 2) if c == 0 else (1,))
         gh_ref[pl.ds(0, HALF), cols] = sum_y(lambda sy: qm[sy, :, cols])
         if c == 0:

time: 59.1 us -> 58.7 us (level)
  no operation moved by 1% of the time
where the time goes in v6:
time: 58.7 us; the launch traced here: 58.5 us
  Pallas kernels  56.6 us (96%)
  between operations  1.93 us (3%)
    pallas_call x1, Pallas kernels, local(): pl.pallas_call(kernel, out_shape=tuple((pltpu.VMEM(a.shape, a.dtype) for...  55.9 us

profile of v6, /device:TPU:1, one launch (start us, length us, event | category | flops | bytes accessed | tf_op | source)
XLA Modules:
  0.0 58.5 jit_solution(13048179055465007956)
XLA Ops:
  1.9 55.9 %contrastive.1 = (bf16[32,1152]{1,0:T(8,128)(2,1)S(1)}, bf16[32,1152]{1,0:T(8,128)(2,1)S(1)}, f32[18,1152]{1,0:T(8,128)S(1)}) custom-call(f32[1]{0:T(128)S(6)} %copy.8.scale_ref, f32[1]{0:T(128)S(6)} %copy.9.bias_ref, bf16[32,1152]{1,0:T(8,128)(2,1)} %image_hbm.1, bf16[32,1152]{1,0:T(8,128)(2,1)} %text_hbm.1, bf16[1152,1152]{1,0:T(8,128)(2,1)} %head_hbm.1), custom_call_target="tpu_custom_call" | custom-call | tf_op jit(solution)/shard_map/contrastive/pallas_call | solution.py:480
  57.8 0.7 %deliver.1 = (bf16[32,1152]{1,0:T(8,128)(2,1)}, bf16[32,1152]{1,0:T(8,128)(2,1)}, f32[18,1152]{1,0:T(8,128)}) custom-call(bf16[32,1152]{1,0:T(8,128)(2,1)S(1)} %get-tuple-element.6.gi_ref, bf16[32,1152]{1,0:T(8,128)(2,1)S(1)} %get-tuple-element.7.gt_ref, f32[18,1152]{1,0:T(8,128)S(1)} %get-tuple-element.8.gh_ref), custom_call_target="tpu_custom_call" | custom-call | tf_op jit(solution)/shard_map/deliver/pallas_call | solution.py:521

commit v7 on v6

--- a/solution.py
+++ b/solution.py
@@ -214,11 +214,10 @@
         cols = pl.ds(*CHUNKS[c])
         cr[(sign, dist, half, c)] = send(
             tp.at[rows(TEXT_ROW[slot] + half * HALF, HALF), cols], rz.at[n, :, cols],
-            1, r_rs1 if dist == 1 else r_rs.at[m], at(dz=sign * (2 if dist == 4 else 1)))
+            1, r_rs1 if dist < 3 else r_rs.at[m], at(dz=sign * (2 if dist in (2, 4) else 1)))
 
     def take_rs(sign, dists, half, c):
-        to = 2 if 4 in dists or 3 in dists else 1
-        slot = to if sign > 0 else 8 - to
+        slot = 2 if sign > 0 else 6
         part = rows(TEXT_ROW[slot] + half * HALF, HALF)
         cols = pl.ds(*CHUNKS[c])
         total = tp[part, cols].astype(F32)
@@ -226,7 +225,7 @@
             cr[(sign, dist, half, c)].wait_recv()
             total = total + rz[rz_slot(sign, dist, half), :, cols].astype(F32)
         tp[part, cols] = total.astype(BF16)
-        ship_rs(sign, to, half, c)
+        ship_rs(sign, 2, half, c)
 
     def image_tile(i):
         part = rows(i * 256, 256)
@@ -266,6 +265,10 @@
             ship_rs(-1, 3, half, c)
     weigh(0, 1)
     tile(0)
+    for c in range(2):
+        for half in range(2):
+            ship_rs(1, 1, half, c)
+            ship_rs(-1, 1, half, c)
     ex = [give_image(0), give_image(1)]
     image_tile(0)
     image_tile(1)
@@ -282,10 +285,6 @@
         for j in range(4):
             ship_ir("by", i, ip.at[rows(256 + j * 64 + i * HALF, HALF), :],
                     iby.at[i - 1, rows(j * HALF, HALF), :], 1, at(dy=i))
-    for c in range(2):
-        for half in range(2):
-            take_rs(1, (2,), half, c)
-            take_rs(-1, (2,), half, c)
     fall[0] = fsel_ref[k * 4 + x]
     for dk in range(2):
         for dx in range(4):
@@ -303,11 +302,13 @@
                 total = total + recv[i, rows(j * HALF, HALF), :].astype(F32)
             ip[part, :] = total.astype(BF16)
 
-    wait_all(rz.at[pl.ds(0, 4)], r_rs1)
+    wait_all(rz.at[pl.ds(0, 8)], r_rs1)
     halves = []
     for half in range(2):
         total = tp[rows(half * HALF, HALF), :].astype(F32)
-        total = total + rz[rz_slot(1, 1, half)].astype(F32) + rz[rz_slot(-1, 1, half)].astype(F32)
+        for dist in (1, 2):
+            for sign in (1, -1):
+                total = total + rz[rz_slot(sign, dist, half)].astype(F32)
         halves.append(total)
     text_sum = jnp.concatenate(halves, axis=0)
     text_dir = tdir[...]
@@ -511,7 +512,7 @@
             V((4, HALF, D), BF16),
             V((4, 2, D), BF16),
             dma((3,)),
-            dma((6,)), dma((6,)), dma, dma((17,)), dma, dma((20,)), dma, dma((2,)), dma((4,)),
+            dma((6,)), dma((6,)), dma, dma((17,)), dma, dma((12,)), dma, dma((2,)), dma((4,)),
             dma((3,)), dma, dma((2,)), dma, dma((12,)), dma((12,)), dma((9,)),
         ],
         compiler_params=pltpu.CompilerParams(

time: 58.7 us -> 57.3 us (0.976)
  Pallas kernels: 56.6 us -> 55.3 us
    pallas_call x1, Pallas kernels: 55.9 us -> 54.5 us  [local(): pl.pallas_call(kernel, out_shape=tuple((pltpu.VMEM(a.shape, a.dtype) for...]
where the time goes in v7:
time: 57.3 us; the launch traced here: 57.2 us
  Pallas kernels  55.3 us (97%)
  between operations  1.93 us (3%)
    pallas_call x1, Pallas kernels, local(): pl.pallas_call(kernel, out_shape=tuple((pltpu.VMEM(a.shape, a.dtype) for...  54.5 us

profile of v7, /device:TPU:1, one launch (start us, length us, event | category | flops | bytes accessed | tf_op | source)
XLA Modules:
  0.0 57.2 jit_solution(10096328306299140332)
XLA Ops:
  1.9 54.5 %contrastive.1 = (bf16[32,1152]{1,0:T(8,128)(2,1)S(1)}, bf16[32,1152]{1,0:T(8,128)(2,1)S(1)}, f32[18,1152]{1,0:T(8,128)S(1)}) custom-call(f32[1]{0:T(128)S(6)} %copy.8.scale_ref, f32[1]{0:T(128)S(6)} %copy.9.bias_ref, bf16[32,1152]{1,0:T(8,128)(2,1)} %image_hbm.1, bf16[32,1152]{1,0:T(8,128)(2,1)} %text_hbm.1, bf16[1152,1152]{1,0:T(8,128)(2,1)} %head_hbm.1), custom_call_target="tpu_custom_call" | custom-call | tf_op jit(solution)/shard_map/contrastive/pallas_call | solution.py:481
  56.5 0.7 %deliver.1 = (bf16[32,1152]{1,0:T(8,128)(2,1)}, bf16[32,1152]{1,0:T(8,128)(2,1)}, f32[18,1152]{1,0:T(8,128)}) custom-call(bf16[32,1152]{1,0:T(8,128)(2,1)S(1)} %get-tuple-element.6.gi_ref, bf16[32,1152]{1,0:T(8,128)(2,1)S(1)} %get-tuple-element.7.gt_ref, f32[18,1152]{1,0:T(8,128)S(1)} %get-tuple-element.8.gh_ref), custom_call_target="tpu_custom_call" | custom-call | tf_op jit(solution)/shard_map/deliver/pallas_call | solution.py:522

commit v8 on v7

--- a/solution.py
+++ b/solution.py
@@ -258,11 +258,12 @@
     weigh(1, 1)
     tile(1)
     for c in range(2):
+        ship_rs(1, 3, 1, c)
+        ship_rs(-1, 3, 0, c)
         ship_rs(1, 4, 0, c)
         ship_rs(-1, 4, 1, c)
-        for half in range(2):
-            ship_rs(1, 3, half, c)
-            ship_rs(-1, 3, half, c)
+        ship_rs(1, 3, 0, c)
+        ship_rs(-1, 3, 1, c)
     weigh(0, 1)
     tile(0)
     for c in range(2):
@@ -273,10 +274,10 @@
     image_tile(0)
     image_tile(1)
     for c in range(2):
+        take_rs(1, (3,), 1, c)
+        take_rs(-1, (3,), 0, c)
         take_rs(1, (4, 3), 0, c)
         take_rs(-1, (4, 3), 1, c)
-        take_rs(1, (3,), 1, c)
-        take_rs(-1, (3,), 0, c)
     join_image(0, ex[0])
     for i in order:
         ship_ir("ay", i, ip.at[rows(i * 64, 64), :], iay.at[i - 1], 0, at(dy=i))

time: 57.3 us -> 57.4 us (level)
  no operation moved by 1% of the time
where the time goes in v8:
time: 57.4 us; the launch traced here: 57.3 us
  Pallas kernels  55.3 us (96%)
  between operations  1.93 us (3%)
    pallas_call x1, Pallas kernels, local(): pl.pallas_call(kernel, out_shape=tuple((pltpu.VMEM(a.shape, a.dtype) for...  54.6 us

profile of v8, /device:TPU:1, one launch (start us, length us, event | category | flops | bytes accessed | tf_op | source)
XLA Modules:
  0.0 57.3 jit_solution(15362378658757360987)
XLA Ops:
  1.9 54.6 %contrastive.1 = (bf16[32,1152]{1,0:T(8,128)(2,1)S(1)}, bf16[32,1152]{1,0:T(8,128)(2,1)S(1)}, f32[18,1152]{1,0:T(8,128)S(1)}) custom-call(f32[1]{0:T(128)S(6)} %copy.8.scale_ref, f32[1]{0:T(128)S(6)} %copy.9.bias_ref, bf16[32,1152]{1,0:T(8,128)(2,1)} %image_hbm.1, bf16[32,1152]{1,0:T(8,128)(2,1)} %text_hbm.1, bf16[1152,1152]{1,0:T(8,128)(2,1)} %head_hbm.1), custom_call_target="tpu_custom_call" | custom-call | tf_op jit(solution)/shard_map/contrastive/pallas_call | solution.py:482
  56.5 0.7 %deliver.1 = (bf16[32,1152]{1,0:T(8,128)(2,1)}, bf16[32,1152]{1,0:T(8,128)(2,1)}, f32[18,1152]{1,0:T(8,128)}) custom-call(bf16[32,1152]{1,0:T(8,128)(2,1)S(1)} %get-tuple-element.6.gi_ref, bf16[32,1152]{1,0:T(8,128)(2,1)S(1)} %get-tuple-element.7.gt_ref, f32[18,1152]{1,0:T(8,128)S(1)} %get-tuple-element.8.gh_ref), custom_call_target="tpu_custom_call" | custom-call | tf_op jit(solution)/shard_map/deliver/pallas_call | solution.py:523

commit v9 on v7

--- a/solution.py
+++ b/solution.py
@@ -175,7 +175,6 @@
             forward_image(2)
             pair(0, 0)
             pair(1, 0)
-            pl.loop(0, 4)(select)
     pl.loop(4, 8)(select)
     for j in (1, 3, 2):
         pair(0, j)
@@ -285,6 +284,7 @@
         for j in range(4):
             ship_ir("by", i, ip.at[rows(256 + j * 64 + i * HALF, HALF), :],
                     iby.at[i - 1, rows(j * HALF, HALF), :], 1, at(dy=i))
+    pl.loop(0, 4)(select)
     fall[0] = fsel_ref[k * 4 + x]
     for dk in range(2):
         for dx in range(4):

time: 57.3 us -> 57.1 us (level)
  no operation moved by 1% of the time
where the time goes in v9:
time: 57.1 us; the launch traced here: 56.9 us
  Pallas kernels  55 us (96%)
  between operations  1.93 us (3%)
    pallas_call x1, Pallas kernels, local(): pl.pallas_call(kernel, out_shape=tuple((pltpu.VMEM(a.shape, a.dtype) for...  54.3 us

profile of v9, /device:TPU:1, one launch (start us, length us, event | category | flops | bytes accessed | tf_op | source)
XLA Modules:
  0.0 56.9 jit_solution(2143839346797470375)
XLA Ops:
  1.9 54.3 %contrastive.1 = (bf16[32,1152]{1,0:T(8,128)(2,1)S(1)}, bf16[32,1152]{1,0:T(8,128)(2,1)S(1)}, f32[18,1152]{1,0:T(8,128)S(1)}) custom-call(f32[1]{0:T(128)S(6)} %copy.8.scale_ref, f32[1]{0:T(128)S(6)} %copy.9.bias_ref, bf16[32,1152]{1,0:T(8,128)(2,1)} %image_hbm.1, bf16[32,1152]{1,0:T(8,128)(2,1)} %text_hbm.1, bf16[1152,1152]{1,0:T(8,128)(2,1)} %head_hbm.1), custom_call_target="tpu_custom_call" | custom-call | tf_op jit(solution)/shard_map/contrastive/pallas_call | solution.py:481
  56.2 0.7 %deliver.1 = (bf16[32,1152]{1,0:T(8,128)(2,1)}, bf16[32,1152]{1,0:T(8,128)(2,1)}, f32[18,1152]{1,0:T(8,128)}) custom-call(bf16[32,1152]{1,0:T(8,128)(2,1)S(1)} %get-tuple-element.6.gi_ref, bf16[32,1152]{1,0:T(8,128)(2,1)S(1)} %get-tuple-element.7.gt_ref, f32[18,1152]{1,0:T(8,128)S(1)} %get-tuple-element.8.gh_ref), custom_call_target="tpu_custom_call" | custom-call | tf_op jit(solution)/shard_map/deliver/pallas_call | solution.py:522
